TPU v7x, 512 devices: a whole 4x4x16 slice. The times are simulated.
512 devices in a mesh: head: 8 (over y, core), seq: 64 (over x, z).
Axes of the slice: x: 4, y: 4, z: 16, core: 2. Of those that a mesh axis runs over, the one named last changes fastest.
Arguments:
- query_vectors: bfloat16 [8192, 4096], P('seq', 'head'), may hold values from -1000 to 1000
- key_vectors: bfloat16 [8192, 4096], P('seq', 'head'), may hold values from -1000 to 1000
- value_vectors: bfloat16 [8192, 4096], P('seq', 'head'), may hold values from -6 to 6
- cluster: int32 [32, 8192], P('head', 'seq'), may hold values from 0 to 127, as said below
- centroids: float32 [32, 128, 128], P('head'), may hold values from -1.25 to 1.25
- upstream: bfloat16 [8192, 4096], P('seq', 'head'), may hold values from -6 to 6
Outputs:
- attended: bfloat16 [8192, 4096], P('seq', 'head')
- grad_queries: bfloat16 [8192, 4096], P('seq', 'head')
- grad_keys: bfloat16 [8192, 4096], P('seq', 'head')
- grad_values: bfloat16 [8192, 4096], P('seq', 'head')
- new_centroids: float32 [32, 128, 128], P('head')
Inputs may be any that keep to these rules, and one draw needn't show every extreme that they name: In every head each cluster holds exactly 64 tokens. Of the 128 tokens of one index of seq at most 2 fall into one cluster of a head, and every cluster of every head receives exactly 2 from some index of seq. In each head the clusters fall into pairs whose counts from one index of seq add up to 2.
All inputs are finite; a program needn't handle non-finite values.
Results may differ from a plain program's by a relative error of at most 0.015.
Values may be sent and summed in bfloat16 or wider, within the bound.
A program may use at most 64 MiB of HBM per device.

v0:
```python
import jax
import jax.numpy as jnp
from jax import lax
from jax.sharding import PartitionSpec as P

MASKED = -1e30
EPSILON = 1e-06
RETAIN = 0.9


def copy_for_each(value, axis):
    peers = lax.axis_size(axis)
    return lax.all_to_all(
        jnp.broadcast_to(value[None], (peers, *value.shape)), axis, 0, 0, tiled=True
    )


def taken_together(value, axis):
    return copy_for_each(value, axis).sum(axis=0)


def in_one(arrays, axis):
    vector, at, done = (jnp.concatenate([a.reshape(-1) for a in arrays]), 0, [])
    running = taken_together(vector, axis)
    for a in arrays:
        done.append(running[at : at + a.size].reshape(a.shape))
        at += a.size
    return tuple(done)


def in_order(tiles, dim):
    shape = list(tiles.shape[1:])
    shape[dim] *= tiles.shape[0]
    return jnp.moveaxis(tiles, 0, dim).reshape(shape)


def collect(value, axis, dim):
    return in_order(copy_for_each(value, axis), dim)


def attend_forward(query_rows, key_rows, value_rows, live_slots):
    factor = query_rows.shape[-1] ** (-0.5)
    places = jnp.arange(query_rows.shape[1], dtype=jnp.int32)
    allowed = (places[None, :] <= places[:, None])[None, :, :] & (live_slots[:, None, :] > 0)
    scores = (
        jnp.einsum("gsd,gtd->gst", query_rows, key_rows, preferred_element_type=jnp.float32)
        * factor
    )
    scores = jnp.where(allowed, scores, MASKED)
    row_max = jnp.max(scores, axis=2, keepdims=True)
    raised = jnp.exp(scores - row_max)
    weights = raised / jnp.sum(raised, axis=2, keepdims=True)
    weights_low = weights.astype(jnp.bfloat16)
    attended = jnp.einsum(
        "gst,gtd->gsd", weights_low, value_rows, preferred_element_type=jnp.float32
    ).astype(jnp.bfloat16)
    return (weights, weights_low, attended)


def attend_backward(
    query_rows, key_rows, value_rows, upstream_rows, weights, weights_low, attended
):
    factor = query_rows.shape[-1] ** (-0.5)
    row_dot = jnp.sum(upstream_rows.astype(jnp.float32) * attended.astype(jnp.float32), axis=2)
    grad_weights = jnp.einsum(
        "gsd,gtd->gst", upstream_rows, value_rows, preferred_element_type=jnp.float32
    )
    grad_scores = (weights * (grad_weights - row_dot[:, :, None]) * factor).astype(jnp.bfloat16)
    grad_query = jnp.einsum(
        "gst,gtd->gsd", grad_scores, key_rows, preferred_element_type=jnp.float32
    ).astype(jnp.bfloat16)
    grad_key = jnp.einsum(
        "gst,gsd->gtd", grad_scores, query_rows, preferred_element_type=jnp.float32
    ).astype(jnp.bfloat16)
    grad_value = jnp.einsum(
        "gst,gsd->gtd", weights_low, upstream_rows, preferred_element_type=jnp.float32
    ).astype(jnp.bfloat16)
    return (grad_query, grad_key, grad_value)


def unit_sums(key_rows, live_slots):
    key_wide = key_rows.astype(jnp.float32)
    unit_keys = key_wide * lax.rsqrt(jnp.sum(key_wide * key_wide, axis=2, keepdims=True) + EPSILON)
    return jnp.sum(unit_keys * live_slots.astype(jnp.float32)[:, :, None], axis=1)


def owner_forward(received):

    def per_item(pieces):
        query_rows, key_rows, value_rows, live_slots = (
            pieces[0][0],
            pieces[1][0],
            pieces[2][0],
            pieces[3][0],
        )
        weights, weights_low, attended = attend_forward(
            query_rows, key_rows, value_rows, live_slots
        )
        return (attended, unit_sums(key_rows, live_slots))

    attended, key_sums = lax.map(per_item, received)
    returned = lax.all_to_all(attended[:, None], "seq", split_axis=3, concat_axis=1, tiled=True)
    return (returned, key_sums)


def owner_backward(received):

    def per_item(pieces):
        query_rows, key_rows, value_rows = (pieces[0][0], pieces[1][0], pieces[2][0])
        upstream_rows, live_slots = (pieces[3][0], pieces[4][0])
        weights, weights_low, attended = attend_forward(
            query_rows, key_rows, value_rows, live_slots
        )
        return attend_backward(
            query_rows, key_rows, value_rows, upstream_rows, weights, weights_low, attended
        )

    grad_query, grad_key, grad_value = lax.map(per_item, received)
    return (
        lax.all_to_all(grad_query[:, None], "seq", split_axis=3, concat_axis=1, tiled=True),
        lax.all_to_all(grad_key[:, None], "seq", split_axis=3, concat_axis=1, tiled=True),
        lax.all_to_all(grad_value[:, None], "seq", split_axis=3, concat_axis=1, tiled=True),
    )


def local(query_vectors, key_vectors, value_vectors, cluster, centroids, upstream):
    tokens_dev, width_dev = query_vectors.shape
    heads_dev = cluster.shape[0]
    clusters = centroids.shape[1]
    head_dim = width_dev // heads_dev
    owners = lax.axis_size("seq")
    per_owner = clusters // owners
    capacity = 2 * (tokens_dev // clusters)
    full_width = width_dev * lax.axis_size("head")
    query_wide = query_vectors.astype(jnp.float32)
    key_wide = key_vectors.astype(jnp.float32)
    query_squares, key_squares = in_one(
        (jnp.sum(query_wide * query_wide, axis=1), jnp.sum(key_wide * key_wide, axis=1)), "head"
    )
    query_scale = lax.rsqrt(query_squares / full_width + EPSILON)
    key_scale = lax.rsqrt(key_squares / full_width + EPSILON)
    query_norm = query_wide * query_scale[:, None]
    key_norm = key_wide * key_scale[:, None]
    query_low = query_norm.astype(jnp.bfloat16)
    key_low = key_norm.astype(jnp.bfloat16)
    member = (cluster[:, :, None] == jnp.arange(clusters, dtype=jnp.int32)[None, None, :]).astype(
        jnp.bfloat16
    )
    token_ids = jnp.arange(tokens_dev, dtype=jnp.int32)
    earlier = (token_ids[None, :] < token_ids[:, None]).astype(jnp.bfloat16)
    before = jnp.einsum("st,htc->hsc", earlier, member, preferred_element_type=jnp.float32)
    position_in = jnp.sum(before * member.astype(jnp.float32), axis=2).astype(jnp.int32)
    slot_index = cluster * capacity + position_in
    head_grid = jnp.arange(heads_dev, dtype=jnp.int32)[:, None]
    holder = jnp.full((heads_dev, clusters * capacity), tokens_dev, jnp.int32)
    holder = holder.at[head_grid, slot_index].set(token_ids[None, :])
    occupied = holder < tokens_dev
    source_row = jnp.minimum(holder, tokens_dev - 1)

    def arrange(rows):
        by_head = rows.reshape(tokens_dev, heads_dev, head_dim)
        picked = by_head[source_row, head_grid]
        picked = jnp.where(occupied[:, :, None], picked, jnp.zeros((), rows.dtype))
        return picked.reshape(heads_dev, owners, per_owner, capacity, head_dim)

    heads_row = jnp.arange(heads_dev, dtype=jnp.int32)[None, :]

    def restore(returned):
        gathered = returned.reshape(heads_dev, clusters * capacity, head_dim)
        return gathered[heads_row, slot_index.T].reshape(tokens_dev, width_dev)

    query_send = arrange(query_low)
    key_send = arrange(key_low)
    value_send = arrange(value_vectors)
    live_send = occupied.astype(jnp.bfloat16).reshape(heads_dev, owners, per_owner, capacity)
    forward_out = owner_forward(
        (
            lax.all_to_all(query_send, "seq", split_axis=1, concat_axis=3, tiled=True),
            lax.all_to_all(key_send, "seq", split_axis=1, concat_axis=3, tiled=True),
            lax.all_to_all(value_send, "seq", split_axis=1, concat_axis=3, tiled=True),
            lax.all_to_all(live_send, "seq", split_axis=1, concat_axis=3, tiled=True),
        )
    )
    upstream_send = arrange(upstream)
    backward_out = owner_backward(
        (
            lax.all_to_all(query_send, "seq", split_axis=1, concat_axis=3, tiled=True),
            lax.all_to_all(key_send, "seq", split_axis=1, concat_axis=3, tiled=True),
            lax.all_to_all(value_send, "seq", split_axis=1, concat_axis=3, tiled=True),
            lax.all_to_all(upstream_send, "seq", split_axis=1, concat_axis=3, tiled=True),
            lax.all_to_all(live_send, "seq", split_axis=1, concat_axis=3, tiled=True),
        )
    )
    attended = restore(forward_out[0])
    grad_query_low = restore(backward_out[0])
    grad_key_low = restore(backward_out[1])
    grad_values = restore(backward_out[2])
    key_sums = forward_out[1]
    query_inner, key_inner = in_one(
        (
            jnp.sum(grad_query_low.astype(jnp.float32) * query_norm, axis=1),
            jnp.sum(grad_key_low.astype(jnp.float32) * key_norm, axis=1),
        ),
        "head",
    )
    grad_queries = (
        query_scale[:, None]
        * (grad_query_low.astype(jnp.float32) - query_norm * (query_inner / full_width)[:, None])
    ).astype(jnp.bfloat16)
    grad_keys = (
        key_scale[:, None]
        * (grad_key_low.astype(jnp.float32) - key_norm * (key_inner / full_width)[:, None])
    ).astype(jnp.bfloat16)
    first_row = lax.axis_index("seq") * per_owner
    current = lax.dynamic_slice_in_dim(centroids, first_row, per_owner, 1)
    blended = RETAIN * current + (1.0 - RETAIN) * key_sums
    renewed = blended * lax.rsqrt(jnp.sum(blended * blended, axis=2, keepdims=True) + EPSILON)
    new_centroids = collect(renewed, "seq", 1)
    return (attended, grad_queries, grad_keys, grad_values, new_centroids)


def solution(mesh):
    placed = (
        P("seq", "head"),
        P("seq", "head"),
        P("seq", "head"),
        P("head", "seq"),
        P("head", None, None),
        P("seq", "head"),
    )
    return jax.shard_map(
        local,
        mesh=mesh,
        in_specs=placed,
        out_specs=(
            P("seq", "head"),
            P("seq", "head"),
            P("seq", "head"),
            P("seq", "head"),
            P("head", None, None),
        ),
        check_vma=False,
    )
```

profile of v0, /device:TPU:6, one launch (start us, length us, event | category | flops | bytes accessed | tf_op | source)
XLA Modules:
  0.0 341.7 jit_solution(8409736779228207290)
XLA Ops:
  0.6 1.1 fusion.93
  2.4 4.5 %all-to-all-start.1 = ((f32[8,1,256]{2,1,0:T(1,128)}), f32[8,1,256]{2,1,0:T(1,128)S(1)}, u32[]{:S(2)}, u32[]{:S(2)}) async-start(f32[8,1,256]{2,1,0:T(1,128)} %broadcast_in_dim.99), calls=%async_computation.1 | async-start | bytes 16384 | tf_op jit(solution)/shard_map/all_to_all | solution.py:13
  7.7 24.7 %scatter_fusion = s32[4,256]{1,0:T(4,128)S(1)} fusion(s32[4,256]{1,0:T(4,128)S(1)} %broadcast.111, s32[512]{0:T(512)S(1)} %fusion.111, s32[512]{0:T(512)S(1)} %iota_bitcast_fusion), kind=kCustom, calls=%fused_computation.8 | custom fusion | bytes 10240 | tf_op jit(solution)/shard_map/scatter | solution.py:156
  33.4 1.7 copy.150
  35.1 0.9 copy-done.3
  36.0 5.8 %gather_fusion.4 = bf16[1024,128]{1,0:T(8,128)(2,1)S(1)} fusion(bf16[128,4,128]{2,1,0:T(4,128)(2,1)S(1)} %reshape.176, s32[1024]{0:T(1024)S(1)} %bitcast.217), kind=kCustom, calls=%fused_computation.4 | custom fusion | bytes 532480 | tf_op jit(solution)/shard_map/gather | solution.py:162
  41.9 5.8 %gather_fusion.2 = bf16[1024,128]{1,0:T(8,128)(2,1)S(1)} fusion(bf16[128,4,128]{2,1,0:T(4,128)(2,1)S(1)} %reshape.173, s32[1024]{0:T(1024)S(1)} %bitcast.218), kind=kCustom, calls=%fused_computation.2 | custom fusion | bytes 532480 | tf_op jit(solution)/shard_map/gather | solution.py:162
  47.7 18.9 %all-to-all-start = ((bf16[4,64,2,2]{0,3,2,1:T(2,128)(2,1)}), bf16[4,64,2,2]{0,3,2,1:T(2,128)(2,1)S(1)}, u32[]{:S(2)}, u32[]{:S(2)}) async-start(bf16[4,64,2,2]{0,3,2,1:T(2,128)(2,1)} %reshape.170), calls=%async_computation | async-start | bytes 131072 | tf_op jit(solution)/shard_map/all_to_all | solution.py:181
  66.9 5.8 %gather_fusion.1 = bf16[1024,128]{1,0:T(8,128)(2,1)S(1)} fusion(bf16[128,4,128]{2,1,0:T(4,128)(2,1)S(1)} %reshape.172, s32[1024]{0:T(1024)S(1)} %bitcast.219), kind=kCustom, calls=%fused_computation.1 | custom fusion | bytes 532480 | tf_op jit(solution)/shard_map/gather | solution.py:162
  72.8 5.8 %gather_fusion = bf16[1024,128]{1,0:T(8,128)(2,1)S(1)} fusion(bf16[128,4,128]{2,1,0:T(4,128)(2,1)S(1)} %reshape.171, s32[1024]{0:T(1024)S(1)} %bitcast.220), kind=kCustom, calls=%fused_computation | custom fusion | bytes 532480 | tf_op jit(solution)/shard_map/gather | solution.py:162
  78.7 2.4 broadcast_select_fusion
  81.0 35.8 %all_to_all.187 = bf16[4,64,2,2,128]{4,3,2,0,1:T(2,128)(2,1)S(1)} all-to-all(bf16[4,64,2,2,128]{4,3,2,0,1:T(2,128)(2,1)S(1)} %get-tuple-element.218), channel_id=1, replica_groups=mesh['head'=8,'seq'=64] {'seq'}, dimensions={1} | all-to-all | bytes 524288 | tf_op jit(solution)/shard_map/all_to_all | solution.py:178
  116.8 26.5 %all_to_all.188 = bf16[4,64,2,2,128]{4,3,2,0,1:T(2,128)(2,1)S(1)} all-to-all(bf16[4,64,2,2,128]{4,3,2,0,1:T(2,128)(2,1)S(1)} %get-tuple-element.216), channel_id=1, replica_groups=mesh['head'=8,'seq'=64] {'seq'}, dimensions={1} | all-to-all | bytes 524288 | tf_op jit(solution)/shard_map/all_to_all | solution.py:179
  143.3 6.6 %all-to-all-start.4 = ((bf16[4,64,2,2,128]{4,3,2,0,1:T(2,128)(2,1)}), bf16[4,64,2,2,128]{4,3,2,0,1:T(2,128)(2,1)S(1)}, u32[]{:S(2)}, u32[]{:S(2)}) async-start(bf16[4,64,2,2,128]{4,3,2,0,1:T(2,128)(2,1)} %get-tuple-element.217), calls=%async_computation.4 | async-start | bytes 524288 | tf_op jit(solution)/shard_map/all_to_all | solution.py:180
  150.5 19.1 %all-to-all-done.4 = bf16[4,64,2,2,128]{4,3,2,0,1:T(2,128)(2,1)S(1)} async-done(((bf16[4,64,2,2,128]{4,3,2,0,1:T(2,128)(2,1)}), bf16[4,64,2,2,128]{4,3,2,0,1:T(2,128)(2,1)S(1)}, u32[]{:S(2)}, u32[]{:S(2)}) %all-to-all-start.4) | async-done | bytes 262176 | tf_op jit(solution)/shard_map/all_to_all | solution.py:180
  169.6 6.6 %all-to-all-start.6 = ((bf16[4,64,2,2,128]{4,3,2,0,1:T(2,128)(2,1)}), bf16[4,64,2,2,128]{4,3,2,0,1:T(2,128)(2,1)S(1)}, u32[]{:S(2)}, u32[]{:S(2)}) async-start(bf16[4,64,2,2,128]{4,3,2,0,1:T(2,128)(2,1)} %get-tuple-element.215), calls=%async_computation.6 | async-start | bytes 524288 | tf_op jit(solution)/shard_map/all_to_all | solution.py:190
  177.2 6.0 %while.26 = (s32[]{:T(128)}, bf16[4,2,128,128]{3,1,0,2:T(2,128)(2,1)}, f32[4,2,128]{2,1,0:T(2,128)S(1)}, bf16[4,1,2,128]{3,2,1,0:T(2,128)(2,1)S(1)}, bf16[4,1,2,...) while((s32[]{:T(128)}, ...), condition=%wide.region_10.11_spmd, body=%wide.region_5.10_spmd.sunk | while | flops 17285504 | bytes 833401 | solution.py:101
  183.2 12.3 %all-to-all-done.6 = bf16[4,64,2,2,128]{4,3,2,0,1:T(2,128)(2,1)S(1)} async-done(((bf16[4,64,2,2,128]{4,3,2,0,1:T(2,128)(2,1)}), bf16[4,64,2,2,128]{4,3,2,0,1:T(2,128)(2,1)S(1)}, u32[]{:S(2)}, u32[]{:S(2)}) %all-to-all-start.6) | async-done | bytes 262176 | tf_op jit(solution)/shard_map/all_to_all | solution.py:190
  195.5 6.8 %all-to-all-start.5 = ((bf16[4,1,2,128,128]{4,2,0,1,3:T(2,128)(2,1)}), bf16[4,1,2,128,128]{4,2,0,1,3:T(2,128)(2,1)S(1)}, u32[]{:S(2)}, u32[]{:S(2)}) async-start(bf16[4,1,2,128,128]{4,2,0,1,3:T(2,128)(2,1)} %bitcast.39), calls=%async_computation.5 | async-start | bytes 524288 | tf_op jit(solution)/shard_map/all_to_all | solution.py:102
  203.7 8.8 %while.27 = (s32[]{:T(128)}, bf16[4,2,128,128]{3,1,0,2:T(2,128)(2,1)S(1)}, bf16[4,2,128,128]{3,1,0,2:T(2,128)(2,1)S(1)}, bf16[4,2,128,128]{3,1,0,2:T(2,128)(2,1)...) while((s32[]{:T(128)}, ...), condition=%wide.region_15.16_spmd, body=%wide.region_11.15_spmd.sunk | while | flops 51069056 | bytes 1943941 | solution.py:118
  212.5 9.2 %all-to-all-done.5 = bf16[4,1,2,128,128]{4,2,0,1,3:T(2,128)(2,1)S(1)} async-done(((bf16[4,1,2,128,128]{4,2,0,1,3:T(2,128)(2,1)}), bf16[4,1,2,128,128]{4,2,0,1,3:T(2,128)(2,1)S(1)}, u32[]{:S(2)}, u32[]{:S(2)}) %all-to-all-start.5) | async-done | bytes 262176 | tf_op jit(solution)/shard_map/all_to_all | solution.py:102
  221.7 25.7 %all_to_all.189 = bf16[4,1,2,128,128]{4,2,0,1,3:T(2,128)(2,1)S(1)} all-to-all(bf16[4,1,2,128,128]{4,2,0,1,3:T(2,128)(2,1)S(1)} %bitcast.236), channel_id=1, replica_groups=mesh['head'=8,'seq'=64] {'seq'}, dimensions={3} | all-to-all | bytes 524288 | tf_op jit(solution)/shard_map/all_to_all | solution.py:120
  247.3 25.8 %all_to_all.190 = bf16[4,1,2,128,128]{4,2,0,1,3:T(2,128)(2,1)S(1)} all-to-all(bf16[4,1,2,128,128]{4,2,0,1,3:T(2,128)(2,1)S(1)} %bitcast.237), channel_id=1, replica_groups=mesh['head'=8,'seq'=64] {'seq'}, dimensions={3} | all-to-all | bytes 524288 | tf_op jit(solution)/shard_map/all_to_all | solution.py:121
  273.2 6.6 %all-to-all-start.10 = ((bf16[4,1,2,128,128]{4,2,0,1,3:T(2,128)(2,1)}), bf16[4,1,2,128,128]{4,2,0,1,3:T(2,128)(2,1)S(1)}, u32[]{:S(2)}, u32[]{:S(2)}) async-start(bf16[4,1,2,128,128]{4,2,0,1,3:T(2,128)(2,1)} %bitcast.61), calls=%async_computation.10 | async-start | bytes 524288 | tf_op jit(solution)/shard_map/all_to_all | solution.py:122
  281.4 17.6 %all-to-all-done.10 = bf16[4,1,2,128,128]{4,2,0,1,3:T(2,128)(2,1)S(1)} async-done(((bf16[4,1,2,128,128]{4,2,0,1,3:T(2,128)(2,1)}), bf16[4,1,2,128,128]{4,2,0,1,3:T(2,128)(2,1)S(1)}, u32[]{:S(2)}, u32[]{:S(2)}) %all-to-all-start.10) | async-done | bytes 262176 | tf_op jit(solution)/shard_map/all_to_all | solution.py:122
  299.7 6.6 %all-to-all-start.11 = ((f32[64,4,2,128]{3,2,1,0:T(2,128)}), f32[64,4,2,128]{3,2,1,0:T(2,128)S(1)}, u32[]{:S(2)}, u32[]{:S(2)}) async-start(f32[64,4,2,128]{3,2,1,0:T(2,128)} %broadcast_in_dim.110), calls=%async_computation.11 | async-start | bytes 524288 | tf_op jit(solution)/shard_map/all_to_all | solution.py:13
  306.8 3.2 gather_fusion.5
  310.4 3.2 gather_fusion.6
  314.0 11.5 %all-to-all-done.11 = f32[64,4,2,128]{3,2,1,0:T(2,128)S(1)} async-done(((f32[64,4,2,128]{3,2,1,0:T(2,128)}), f32[64,4,2,128]{3,2,1,0:T(2,128)S(1)}, u32[]{:S(2)}, u32[]{:S(2)}) %all-to-all-start.11) | async-done | bytes 262176 | tf_op jit(solution)/shard_map/all_to_all | solution.py:13
  326.2 4.7 %all-to-all-start.9 = ((f32[8,1,256]{2,1,0:T(1,128)}), f32[8,1,256]{2,1,0:T(1,128)S(1)}, u32[]{:S(2)}, u32[]{:S(2)}) async-start(f32[8,1,256]{2,1,0:T(1,128)} %broadcast_in_dim.108), calls=%async_computation.9 | async-start | bytes 16384 | tf_op jit(solution)/shard_map/all_to_all | solution.py:13
  331.2 3.2 gather_fusion.3
  335.4 3.2 gather_fusion.7
  (147 shorter events, 28.9 us)
Async XLA Ops:
  2.4 45.4 %all-to-all-start.1 = ((f32[8,1,256]{2,1,0:T(1,128)}), f32[8,1,256]{2,1,0:T(1,128)S(1)}, u32[]{:S(2)}, u32[]{:S(2)}) async-start(f32[8,1,256]{2,1,0:T(1,128)} %broadcast_in_dim.99), calls=%async_computation.1 | async-start | bytes 16384 | tf_op jit(solution)/shard_map/all_to_all | solution.py:13
  6.8 0.7 copy-start.4
  33.4 1.7 copy-start.2
  35.1 0.9 copy-start.3
  47.7 19.0 %copy-start.1 = (bf16[128,512]{1,0:T(8,128)(2,1)S(1)}, bf16[128,512]{1,0:T(8,128)(2,1)}, u32[]{:S(2)}) copy-start(bf16[128,512]{1,0:T(8,128)(2,1)} %param.11) | copy-start | bytes 393220
  47.7 33.3 %all-to-all-start = ((bf16[4,64,2,2]{0,3,2,1:T(2,128)(2,1)}), bf16[4,64,2,2]{0,3,2,1:T(2,128)(2,1)S(1)}, u32[]{:S(2)}, u32[]{:S(2)}) async-start(bf16[4,64,2,2]{0,3,2,1:T(2,128)(2,1)} %reshape.170), calls=%async_computation | async-start | bytes 131072 | tf_op jit(solution)/shard_map/all_to_all | solution.py:181
  66.8 5.8 %copy-start = (bf16[128,512]{1,0:T(8,128)(2,1)S(1)}, bf16[128,512]{1,0:T(8,128)(2,1)}, u32[]{:S(2)}) copy-start(bf16[128,512]{1,0:T(8,128)(2,1)} %param.10) | copy-start | bytes 393220
  143.3 26.3 %all-to-all-start.4 = ((bf16[4,64,2,2,128]{4,3,2,0,1:T(2,128)(2,1)}), bf16[4,64,2,2,128]{4,3,2,0,1:T(2,128)(2,1)S(1)}, u32[]{:S(2)}, u32[]{:S(2)}) async-start(bf16[4,64,2,2,128]{4,3,2,0,1:T(2,128)(2,1)} %get-tuple-element.217), calls=%async_computation.4 | async-start | bytes 524288 | tf_op jit(solution)/shard_map/all_to_all | solution.py:180
  169.6 25.9 %all-to-all-start.6 = ((bf16[4,64,2,2,128]{4,3,2,0,1:T(2,128)(2,1)}), bf16[4,64,2,2,128]{4,3,2,0,1:T(2,128)(2,1)S(1)}, u32[]{:S(2)}, u32[]{:S(2)}) async-start(bf16[4,64,2,2,128]{4,3,2,0,1:T(2,128)(2,1)} %get-tuple-element.215), calls=%async_computation.6 | async-start | bytes 524288 | tf_op jit(solution)/shard_map/all_to_all | solution.py:190
  195.5 26.1 %all-to-all-start.5 = ((bf16[4,1,2,128,128]{4,2,0,1,3:T(2,128)(2,1)}), bf16[4,1,2,128,128]{4,2,0,1,3:T(2,128)(2,1)S(1)}, u32[]{:S(2)}, u32[]{:S(2)}) async-start(bf16[4,1,2,128,128]{4,2,0,1,3:T(2,128)(2,1)} %bitcast.39), calls=%async_computation.5 | async-start | bytes 524288 | tf_op jit(solution)/shard_map/all_to_all | solution.py:102
  273.2 25.8 %all-to-all-start.10 = ((bf16[4,1,2,128,128]{4,2,0,1,3:T(2,128)(2,1)}), bf16[4,1,2,128,128]{4,2,0,1,3:T(2,128)(2,1)S(1)}, u32[]{:S(2)}, u32[]{:S(2)}) async-start(bf16[4,1,2,128,128]{4,2,0,1,3:T(2,128)(2,1)} %bitcast.61), calls=%async_computation.10 | async-start | bytes 524288 | tf_op jit(solution)/shard_map/all_to_all | solution.py:122
  299.7 25.8 %all-to-all-start.11 = ((f32[64,4,2,128]{3,2,1,0:T(2,128)}), f32[64,4,2,128]{3,2,1,0:T(2,128)S(1)}, u32[]{:S(2)}, u32[]{:S(2)}) async-start(f32[64,4,2,128]{3,2,1,0:T(2,128)} %broadcast_in_dim.110), calls=%async_computation.11 | async-start | bytes 524288 | tf_op jit(solution)/shard_map/all_to_all | solution.py:13
  326.2 13.9 %all-to-all-start.9 = ((f32[8,1,256]{2,1,0:T(1,128)}), f32[8,1,256]{2,1,0:T(1,128)S(1)}, u32[]{:S(2)}, u32[]{:S(2)}) async-start(f32[8,1,256]{2,1,0:T(1,128)} %broadcast_in_dim.108), calls=%async_computation.9 | async-start | bytes 16384 | tf_op jit(solution)/shard_map/all_to_all | solution.py:13
where the time goes:
time: 344 us; the launch traced here: 342 us
  blocking collectives  114 us (33%)
  local copies, waits for them, and re-layouts  79.3 us (23%)
  waiting for transfers between devices  69.7 us (20%)
  starting transfers between devices  61.3 us (18%)
  other arithmetic  9.27 us (3%)
  matrix products  6.98 us (2%)
    all_to_all x1, blocking collectives, local(): lax.all_to_all(query_send, 'seq', split_axis=1, concat_axis=3, tiled=True)  35.8 us
    all_to_all x1, blocking collectives, local(): lax.all_to_all(key_send, 'seq', split_axis=1, concat_axis=3, tiled=True)  26.5 us
    all_to_all x1, blocking collectives, owner_backward(): lax.all_to_all(grad_key[:, None], 'seq', split_axis=3, concat_axis=1, til...  25.8 us
    all_to_all x1, blocking collectives, owner_backward(): lax.all_to_all(grad_query[:, None], 'seq', split_axis=3, concat_axis=1, t...  25.7 us
    scatter x1, local copies, waits for them, and re-layouts, local(): holder = holder.at[head_grid, slot_index].set(token_ids[None, :])  24.7 us
    gather x4, local copies, waits for them, and re-layouts, arrange(): picked = by_head[source_row, head_grid]  23.3 us
    all_to_all x1, waiting for transfers between devices, local(): lax.all_to_all(value_send, 'seq', split_axis=1, concat_axis=3, tiled=True)  19.1 us
    all_to_all x1, starting transfers between devices, local(): lax.all_to_all(live_send, 'seq', split_axis=1, concat_axis=3, tiled=True)  18.9 us
  transfers between devices with their start and end apart: 8, of which 5 were waited for; matrix products, arithmetic and copies ran while one was open for 26% of the time, Pallas kernels for 0%

commit v1 on v0

v1 whole, which is shorter than its diff:
```python
import functools

import jax
import jax.numpy as jnp
from jax import lax
from jax.experimental import pallas as pl
from jax.experimental.pallas import tpu as pltpu
from jax.sharding import PartitionSpec as P

MASKED = -1e30
EPSILON = 1e-06
RETAIN = 0.9
MESH = pl.DeviceIdType.MESH
F32 = jnp.float32
BF16 = jnp.bfloat16

HD = 128
NS = 64
NX, NZ = 4, 16
NH = 8
HL = 4
T = 128
C = 128
WIDTH = 4096
ROWS = NS * 8


def iota(shape, dim):
    return lax.broadcasted_iota(jnp.int32, shape, dim)


def nt(a, b):
    return lax.dot_general(a, b, (((1,), (1,)), ((), ())), preferred_element_type=F32)


def tn(a, b):
    return lax.dot_general(a, b, (((0,), (0,)), ((), ())), preferred_element_type=F32)


def nn(a, b):
    return lax.dot_general(a, b, (((1,), (0,)), ((), ())), preferred_element_type=F32)


def to_row(column, eye):
    return jnp.sum(eye * column, axis=0, keepdims=True)


def to_col(row, eye):
    return jnp.sum(eye * row, axis=1, keepdims=True)


def peer_of(i, me):
    x, z = me // NZ, me % NZ
    e, j = i // NZ, i % NZ
    far = NZ // 2 - (j + 1) // 2
    dz = far * (2 * (j % 2) - 1) + NZ
    dx = NX - 1 - e
    return ((x + dx) % NX) * NZ + (z + dz) % NZ


def kernel(
    q_hbm, k_hbm, v_hbm, u_hbm, cl_hbm, cen_hbm,
    att_o, gq_o, gk_o, gv_o, cen_o,
    q_s, k_s, v_s, u_s, cl_s, cen_s,
    xs, qn_s, kn_s, gql_s, gkl_s, perm, permt, oht,
    sq_send, sq_recv, in_send, in_recv, cnt_send, cnt_recv, cen_send, cen_recv,
    f_send, f_recv, b_send, b_recv,
    load_sem, sq_ss, sq_rs, in_ss, in_rs, cnt_ss, cnt_rs, cen_ss, cen_rs,
    f_ss, f_rs, b_ss, b_rs,
):
    me = lax.axis_index("seq")
    hme = lax.axis_index("head")

    loads = [
        pltpu.make_async_copy(src, dst, load_sem.at[n])
        for n, (src, dst) in enumerate(
            ((cl_hbm, cl_s), (q_hbm, q_s), (k_hbm, k_s), (v_hbm, v_s), (u_hbm, u_s), (cen_hbm, cen_s))
        )
    ]
    for load in loads:
        load.start()

    barrier = pltpu.get_barrier_semaphore()

    def greet(i, carry):
        pl.semaphore_signal(barrier, 1, device_id=(hme, peer_of(i, me)), device_id_type=MESH)
        return carry

    lax.fori_loop(0, NS - 1, greet, 0)

    def greet_head(i, carry):
        pl.semaphore_signal(barrier, 1, device_id=((hme + 1 + i) % NH, me), device_id_type=MESH)
        return carry

    lax.fori_loop(0, NH - 1, greet_head, 0)

    def send_all(src_at, dst, ss, rs):
        def step(i, carry):
            p = peer_of(i, me)
            pltpu.make_async_remote_copy(
                src_ref=src_at(p), dst_ref=dst.at[me], send_sem=ss, recv_sem=rs,
                device_id=(hme, p), device_id_type=MESH,
            ).start()
            return carry

        lax.fori_loop(0, NS - 1, step, 0)

    def send_heads(src, dst, ss, rs):
        def step(i, carry):
            pltpu.make_async_remote_copy(
                src_ref=src, dst_ref=dst.at[hme], send_sem=ss, recv_sem=rs,
                device_id=((hme + 1 + i) % NH, me), device_id_type=MESH,
            ).start()
            return carry

        lax.fori_loop(0, NH - 1, step, 0)

    def wait_blocks(buf, n, sem):
        part = buf.at[pl.ds(0, n)]
        pltpu.make_async_copy(part, part, sem).wait()

    ic = iota((T, T), 0)
    il = iota((T, T), 1)
    eye = (ic == il).astype(F32)
    before = (ic < il).astype(F32)
    after = (ic > il).astype(F32)

    loads[0].wait()
    member, cnt_col, earlier, cnt_rows = [], [], [], []
    for h in range(HL):
        m = (ic == cl_s[h : h + 1, :]).astype(F32)
        member.append(m)
        mb = m.astype(BF16)
        n = jnp.sum(m, axis=1, keepdims=True)
        cnt_col.append(n)
        cnt_rows.append(to_row(n, eye))
        earlier.append(jnp.sum(tn(mb, mb) * before, axis=0, keepdims=True))
    cnt_own = jnp.concatenate(cnt_rows + [jnp.zeros((8 - HL, C), F32)], axis=0).astype(BF16)
    cnt_send[...] = cnt_own
    cnt_recv[me] = cnt_own

    loads[1].wait()
    loads[2].wait()
    qf = q_s[...].astype(F32)
    q_row = to_row(jnp.sum(qf * qf, axis=1, keepdims=True), eye)
    kf = k_s[...].astype(F32)
    k_row = to_row(jnp.sum(kf * kf, axis=1, keepdims=True), eye)
    sq_own = jnp.concatenate([q_row, k_row, jnp.zeros((6, T), F32)], axis=0)
    sq_send[...] = sq_own
    sq_recv[hme] = sq_own

    big_r = iota((ROWS, ROWS), 0)
    big_l = iota((ROWS, ROWS), 1)
    perm[...] = (big_r == ((big_l // 2) % 4) * T + (big_l // 8) * 2 + big_l % 2).astype(F32).astype(BF16)
    permt[...] = (big_l == ((big_r // 2) % 4) * T + (big_r // 8) * 2 + big_r % 2).astype(F32).astype(BF16)

    loads[3].wait()
    loads[4].wait()
    for h in range(HL):
        xs[h, 2 * T : 3 * T, :] = v_s[:, h * HD : (h + 1) * HD]
        xs[h, 3 * T : 4 * T, :] = u_s[:, h * HD : (h + 1) * HD]
    loads[5].wait()

    pl.semaphore_wait(barrier, NS - 1 + NH - 1)
    send_heads(sq_send, sq_recv, sq_ss, sq_rs)
    send_all(lambda p: cnt_send, cnt_recv, cnt_ss, cnt_rs)

    wait_blocks(sq_recv, NH - 1, sq_rs)
    squares = jnp.sum(sq_recv[...], axis=0)
    scales = lax.rsqrt(squares * (1.0 / WIDTH) + EPSILON)
    q_scale = to_col(scales[0:1, :], eye)
    k_scale = to_col(scales[1:2, :], eye)
    q_norm = q_s[...].astype(F32) * q_scale
    k_norm = k_s[...].astype(F32) * k_scale
    qn_s[...] = q_norm
    kn_s[...] = k_norm
    q_low = q_norm.astype(BF16)
    k_low = k_norm.astype(BF16)
    for h in range(HL):
        xs[h, 0:T, :] = q_low[:, h * HD : (h + 1) * HD]
        xs[h, T : 2 * T, :] = k_low[:, h * HD : (h + 1) * HD]

    wait_blocks(cnt_recv, NS - 1, cnt_rs)
    table = cnt_recv[...].astype(F32).reshape(ROWS, C).astype(BF16)
    slot = (iota((T, 1), 0) % 2).astype(F32)
    label_col, label_row, pick_lead, pick_other, renewed_at, place_col = [], [], [], [], [], []
    mine = me.astype(F32)
    for h in range(HL):
        spread = (iota((T, ROWS), 1) == (iota((T, ROWS), 0) // 2) * 8 + h).astype(F32).astype(BF16)
        counts = nn(spread, table)
        swing = counts - 1.0
        sb = swing.astype(BF16)
        gram = tn(sb, sb)
        n_row = jnp.sum(swing * swing, axis=0, keepdims=True)
        n_sum = n_row + to_col(n_row, eye)
        opposite = (n_sum + 2.0 * gram == 0.0).astype(F32)
        same = (n_sum - 2.0 * gram == 0.0).astype(F32)
        rank_row = jnp.sum(same * before, axis=0, keepdims=True)
        rank_col = jnp.sum(same * after, axis=1, keepdims=True)
        partner = jnp.where(rank_row == rank_col, opposite, 0.0)
        other_row = jnp.sum(partner * before, axis=0, keepdims=True)
        other_col = jnp.sum(partner * after, axis=1, keepdims=True)
        lead_rank_row = jnp.sum((1.0 - other_col) * before, axis=0, keepdims=True)
        lead_rank_col = jnp.sum((1.0 - other_row) * after, axis=1, keepdims=True)
        partner_rank_col = jnp.sum(partner * lead_rank_row, axis=1, keepdims=True)
        owner_col = jnp.where(other_col > 0.0, partner_rank_col, lead_rank_col)
        base = 8.0 * owner_col + other_col * (2.0 - cnt_col[h])
        place = jnp.sum(member[h] * base, axis=0, keepdims=True) + earlier[h]
        place_col.append(to_col(place, eye))
        target = jnp.concatenate([place + 2.0 * a for a in range(4)], axis=1).astype(jnp.int32)
        onehot = (big_r == target).astype(F32).astype(BF16)
        packed = nn(onehot, xs[h])
        f_send[h] = packed.reshape(NS, 8, HD).astype(BF16)
        f_recv[h, me] = f_send[h, me]
        send_all(lambda p: f_send.at[h, p], f_recv.at[h], f_ss.at[h], f_rs.at[h])
        lead_mine_row = jnp.where((other_row == 0.0) & (lead_rank_row == mine), 1.0, 0.0)
        lead_count = jnp.sum(counts * lead_mine_row, axis=1, keepdims=True)
        label = (slot < lead_count).astype(F32)
        label_col.append(label)
        label_row.append(to_row(label, eye))
        pick_lead.append(jnp.where((other_col == 0.0) & (owner_col == mine), 1.0, 0.0))
        pick_other.append(jnp.where((other_col > 0.0) & (owner_col == mine), 1.0, 0.0))
        renewed_at.append((owner_col * 8.0 + (2.0 * h) + other_col).astype(jnp.int32))

    for h in range(HL):
        for a in range(4):
            oht[h, a * T : (a + 1) * T, :] = (
                (iota((T, ROWS), 1) == (place_col[h] + 2.0 * a).astype(jnp.int32)).astype(F32).astype(BF16)
            )

    factor = HD ** (-0.5)
    causal = il <= ic
    renewed_rows = []
    for h in range(HL):
        wait_blocks(f_recv.at[h], NS - 1, f_rs.at[h])
        received = f_recv[h].astype(F32).reshape(ROWS, HD).astype(BF16)
        rows = nn(perm[...], received)
        k_wide = rows[T : 2 * T]
        u_wide = rows[3 * T : 4 * T]
        low = rows.astype(BF16)
        qr, kr, vr, ur = (low[a * T : (a + 1) * T] for a in range(4))
        allowed = causal & (label_col[h] == label_row[h])
        scores = jnp.where(allowed, nt(qr, kr) * factor, MASKED)
        raised = jnp.exp(scores - jnp.max(scores, axis=1, keepdims=True))
        weights = raised / jnp.sum(raised, axis=1, keepdims=True)
        weights_low = weights.astype(BF16)
        attended = nn(weights_low, vr).astype(BF16)
        row_dot = jnp.sum(u_wide * attended.astype(F32), axis=1, keepdims=True)
        grad_weights = nt(ur, vr)
        grad_scores = (weights * (grad_weights - row_dot) * factor).astype(BF16)
        grad_q = nn(grad_scores, kr).astype(BF16)
        grad_k = tn(grad_scores, qr).astype(BF16)
        grad_v = tn(weights_low, ur).astype(BF16)
        back = nn(permt[...], jnp.concatenate([attended, grad_q, grad_k, grad_v], axis=0))
        b_send[h] = back.reshape(NS, 8, HD).astype(BF16)
        b_recv[h, me] = b_send[h, me]
        send_all(lambda p: b_send.at[h, p], b_recv.at[h], b_ss.at[h], b_rs.at[h])
        unit = k_wide * lax.rsqrt(jnp.sum(k_wide * k_wide, axis=1, keepdims=True) + EPSILON)
        lead_sum = jnp.sum(unit * label_col[h], axis=0, keepdims=True)
        other_sum = jnp.sum(unit * (1.0 - label_col[h]), axis=0, keepdims=True)
        current = cen_s[h]
        for chosen, total in ((pick_lead[h], lead_sum), (pick_other[h], other_sum)):
            blended = RETAIN * jnp.sum(current * chosen, axis=0, keepdims=True) + (1.0 - RETAIN) * total
            renewed_rows.append(
                blended * lax.rsqrt(jnp.sum(blended * blended, axis=1, keepdims=True) + EPSILON)
            )
    cen_own = jnp.concatenate(renewed_rows, axis=0).astype(BF16)
    cen_send[...] = cen_own
    cen_recv[me] = cen_own
    send_all(lambda p: cen_send, cen_recv, cen_ss, cen_rs)

    q_inner = jnp.zeros((T, 1), F32)
    k_inner = jnp.zeros((T, 1), F32)
    for h in range(HL):
        cols = slice(h * HD, (h + 1) * HD)
        wait_blocks(b_recv.at[h], NS - 1, b_rs.at[h])
        received = b_recv[h].astype(F32).reshape(ROWS, HD).astype(BF16)
        home = nn(oht[h], received)
        att_o[:, cols] = home[0:T].astype(BF16)
        gv_o[:, cols] = home[3 * T : 4 * T].astype(BF16)
        gql_s[:, cols] = home[T : 2 * T]
        gkl_s[:, cols] = home[2 * T : 3 * T]
        q_inner += jnp.sum(home[T : 2 * T] * qn_s[:, cols], axis=1, keepdims=True)
        k_inner += jnp.sum(home[2 * T : 3 * T] * kn_s[:, cols], axis=1, keepdims=True)
    in_own = jnp.concatenate([to_row(q_inner, eye), to_row(k_inner, eye), jnp.zeros((6, T), F32)], axis=0)
    in_send[...] = in_own
    in_recv[hme] = in_own
    send_heads(in_send, in_recv, in_ss, in_rs)

    wait_blocks(cen_recv, NS - 1, cen_rs)
    renewed = cen_recv[...].astype(F32).reshape(ROWS, HD).astype(BF16)
    for h in range(HL):
        gather = (iota((C, ROWS), 1) == renewed_at[h]).astype(F32).astype(BF16)
        cen_o[h] = nn(gather, renewed)

    wait_blocks(in_recv, NH - 1, in_rs)
    inner = jnp.sum(in_recv[...], axis=0) * (1.0 / WIDTH)
    q_in = to_col(inner[0:1, :], eye)
    k_in = to_col(inner[1:2, :], eye)
    gq_o[...] = (q_scale * (gql_s[...] - qn_s[...] * q_in)).astype(BF16)
    gk_o[...] = (k_scale * (gkl_s[...] - kn_s[...] * k_in)).astype(BF16)

    wait_blocks(sq_recv, NH - 1, sq_ss)
    wait_blocks(in_recv, NH - 1, in_ss)
    wait_blocks(cnt_recv, NS - 1, cnt_ss)
    wait_blocks(cen_recv, NS - 1, cen_ss)
    for h in range(HL):
        wait_blocks(f_send.at[h], NS - 1, f_ss.at[h])
        wait_blocks(b_send.at[h], NS - 1, b_ss.at[h])


def local(query_vectors, key_vectors, value_vectors, cluster, centroids, upstream):
    wide = (T, HL * HD)
    blocks = (HL, NS, 8, HD)
    dma = pltpu.SemaphoreType.DMA
    return pl.pallas_call(
        kernel,
        out_shape=tuple(jax.ShapeDtypeStruct(wide, BF16) for _ in range(4))
        + (jax.ShapeDtypeStruct((HL, C, HD), F32),),
        in_specs=[pl.BlockSpec(memory_space=pl.ANY)] * 6,
        out_specs=tuple([pl.BlockSpec(memory_space=pltpu.VMEM)] * 5),
        scratch_shapes=[
            pltpu.VMEM(wide, BF16), pltpu.VMEM(wide, BF16), pltpu.VMEM(wide, BF16), pltpu.VMEM(wide, BF16),
            pltpu.VMEM((HL, T), jnp.int32), pltpu.VMEM((HL, C, HD), F32),
            pltpu.VMEM((HL, 4 * T, HD), BF16), pltpu.VMEM(wide, F32), pltpu.VMEM(wide, F32),
            pltpu.VMEM(wide, F32), pltpu.VMEM(wide, F32),
            pltpu.VMEM((ROWS, ROWS), BF16), pltpu.VMEM((ROWS, ROWS), BF16), pltpu.VMEM((HL, ROWS, ROWS), BF16),
            pltpu.VMEM((8, T), F32), pltpu.VMEM((NH, 8, T), F32),
            pltpu.VMEM((8, T), F32), pltpu.VMEM((NH, 8, T), F32),
            pltpu.VMEM((8, C), BF16), pltpu.VMEM((NS, 8, C), BF16),
            pltpu.VMEM((8, HD), BF16), pltpu.VMEM((NS, 8, HD), BF16),
            pltpu.VMEM(blocks, BF16), pltpu.VMEM(blocks, BF16), pltpu.VMEM(blocks, BF16), pltpu.VMEM(blocks, BF16),
            dma((6,)), dma, dma, dma, dma, dma, dma, dma, dma,
            dma((HL,)), dma((HL,)), dma((HL,)), dma((HL,)),
        ],
        compiler_params=pltpu.CompilerParams(collective_id=0, has_side_effects=True),
    )(query_vectors, key_vectors, value_vectors, upstream, cluster, centroids)


def solution(mesh):
    placed = (
        P("seq", "head"),
        P("seq", "head"),
        P("seq", "head"),
        P("head", "seq"),
        P("head", None, None),
        P("seq", "head"),
    )
    return jax.shard_map(
        local,
        mesh=mesh,
        in_specs=placed,
        out_specs=(
            P("seq", "head"),
            P("seq", "head"),
            P("seq", "head"),
            P("seq", "head"),
            P("head", None, None),
        ),
        check_vma=False,
    )
```

time: 344 us -> 93.6 us (0.27)
  the two profiles are of different devices: /device:TPU:6 before, /device:TPU:1 now
where the time goes in v1:
time: 93.6 us; the launch traced here: 93.4 us
  Pallas kernels  88.2 us (94%)
  local copies, waits for them, and re-layouts  4.58 us (5%)
    pallas_call x1, Pallas kernels, local(): pl.pallas_call(kernel, out_shape=tuple((jax.ShapeDtypeStruct(wide, BF16)...  88.2 us
    unnamed x13, local copies, waits for them, and re-layouts  4.58 us

profile of v1, /device:TPU:1, one launch (start us, length us, event | category | flops | bytes accessed | tf_op | source)
XLA Modules:
  0.0 93.4 jit_solution(9298139378693008814)
XLA Ops:
  0.6 88.2 %shard_map.101 = (bf16[128,512]{1,0:T(8,128)(2,1)}, bf16[128,512]{1,0:T(8,128)(2,1)}, bf16[128,512]{1,0:T(8,128)(2,1)}, bf16[128,512]{1,0:T(8,128)(2,1)}, f32[4,128,128]{2,1,0:T(8,128)}) custom-call(bf16[128,512]{1,0:T(8,128)(2,1)} %q_hbm.1, bf16[128,512]{1,0:T(8,128)(2,1)} %k_hbm.1, bf16[128,512]{1,0:T(8,128)(2,1)} %v_hbm.1, bf16[128,512]{1,0:T(8,128)(2,1)} %u_hbm.1, ...), custom_call_target="tpu_custom_call" | custom-call | tf_op jit(solution)/shard_map/pallas_call | solution.py:316
  88.8 0.0 copy-start.3
  88.8 1.6 %copy.16 = bf16[128,512]{1,0:T(8,128)(2,1)} copy(bf16[128,512]{1,0:T(8,128)(2,1)} %get-tuple-element.10) | data formatting | bytes 262144
  90.4 0.0 copy-done.3
  90.5 0.0 copy-start.2
  90.5 0.0 copy-start.1
  90.5 0.7 copy.17
  91.1 0.3 copy-done.2
  91.4 0.0 copy-start
  91.4 0.7 copy.18
  92.1 0.0 copy-done.1
  92.1 0.7 copy.19
  92.7 0.0 copy-done
  92.7 0.7 copy.20
Async XLA Ops:
  88.8 1.6 %copy-start.3 = (bf16[128,512]{1,0:T(8,128)(2,1)S(1)}, bf16[128,512]{1,0:T(8,128)(2,1)}, u32[]{:S(2)}) copy-start(bf16[128,512]{1,0:T(8,128)(2,1)} %get-tuple-element.11) | copy-start | bytes 393220
  90.5 1.0 %copy-start.2 = (bf16[128,512]{1,0:T(8,128)(2,1)S(1)}, bf16[128,512]{1,0:T(8,128)(2,1)}, u32[]{:S(2)}) copy-start(bf16[128,512]{1,0:T(8,128)(2,1)} %get-tuple-element.12) | copy-start | bytes 393220
  90.5 1.6 %copy-start.1 = (bf16[128,512]{1,0:T(8,128)(2,1)S(1)}, bf16[128,512]{1,0:T(8,128)(2,1)}, u32[]{:S(2)}) copy-start(bf16[128,512]{1,0:T(8,128)(2,1)} %get-tuple-element.13) | copy-start | bytes 393220
  91.4 1.3 %copy-start = (f32[4,128,128]{2,1,0:T(8,128)S(1)}, f32[4,128,128]{2,1,0:T(8,128)}, u32[]{:S(2)}) copy-start(f32[4,128,128]{2,1,0:T(8,128)} %get-tuple-element.14) | copy-start | bytes 786436

commit v2 on v1

--- a/solution.py
+++ b/solution.py
@@ -49,27 +49,43 @@
     return jnp.sum(eye * row, axis=1, keepdims=True)
 
 
-def peer_of(i, me):
-    x, z = me // NZ, me % NZ
-    e, j = i // NZ, i % NZ
-    far = NZ // 2 - (j + 1) // 2
-    dz = far * (2 * (j % 2) - 1) + NZ
-    dx = NX - 1 - e
-    return ((x + dx) % NX) * NZ + (z + dz) % NZ
-
-
 def kernel(
     q_hbm, k_hbm, v_hbm, u_hbm, cl_hbm, cen_hbm,
     att_o, gq_o, gk_o, gv_o, cen_o,
     q_s, k_s, v_s, u_s, cl_s, cen_s,
     xs, qn_s, kn_s, gql_s, gkl_s, perm, permt, oht,
     sq_send, sq_recv, in_send, in_recv, cnt_send, cnt_recv, cen_send, cen_recv,
-    f_send, f_recv, b_send, b_recv,
-    load_sem, sq_ss, sq_rs, in_ss, in_rs, cnt_ss, cnt_rs, cen_ss, cen_rs,
-    f_ss, f_rs, b_ss, b_rs,
+    f_send, f_recv, b_send, b_recv, w_send, w_recv,
+    load_sem, sq_ss, sq_rs, in_ss, in_rs, cnt_ss, cnt_rs, cen_ss, cen_rs, cex_ss, cex_rs,
+    f_ss, f_rs, b_ss, b_rs, w_ss, w_rs,
 ):
     me = lax.axis_index("seq")
     hme = lax.axis_index("head")
+    my_x, my_z = me // NZ, me % NZ
+    row_of = [((my_x + NX - 1 - e) % NX) * NZ for e in range(NX)]
+
+    def each_peer(act):
+        def step(j, carry):
+            far = NZ // 2 - (j + 1) // 2
+            z = (my_z + far * (2 * (j % 2) - 1) + NZ) % NZ
+            for e in range(NX):
+                act(row_of[e] + z)
+            return carry
+
+        lax.fori_loop(0, NZ - 1, step, 0)
+        for e in range(NX - 1):
+            act(row_of[e] + my_z)
+
+    def each_head(act):
+        def step(i, carry):
+            act((hme + 1 + i) % NH)
+            return carry
+
+        lax.fori_loop(0, NH - 1, step, 0)
+
+    barrier = pltpu.get_barrier_semaphore()
+    each_peer(lambda p: pl.semaphore_signal(barrier, 1, device_id=(hme, p), device_id_type=MESH))
+    each_head(lambda p: pl.semaphore_signal(barrier, 1, device_id=(p, me), device_id_type=MESH))
 
     loads = [
         pltpu.make_async_copy(src, dst, load_sem.at[n])
@@ -80,40 +96,16 @@
     for load in loads:
         load.start()
 
-    barrier = pltpu.get_barrier_semaphore()
-
-    def greet(i, carry):
-        pl.semaphore_signal(barrier, 1, device_id=(hme, peer_of(i, me)), device_id_type=MESH)
-        return carry
-
-    lax.fori_loop(0, NS - 1, greet, 0)
-
-    def greet_head(i, carry):
-        pl.semaphore_signal(barrier, 1, device_id=((hme + 1 + i) % NH, me), device_id_type=MESH)
-        return carry
-
-    lax.fori_loop(0, NH - 1, greet_head, 0)
+    def send(src, dst, ss, rs, to):
+        pltpu.make_async_remote_copy(
+            src_ref=src, dst_ref=dst, send_sem=ss, recv_sem=rs, device_id=to, device_id_type=MESH
+        ).start()
 
     def send_all(src_at, dst, ss, rs):
-        def step(i, carry):
-            p = peer_of(i, me)
-            pltpu.make_async_remote_copy(
-                src_ref=src_at(p), dst_ref=dst.at[me], send_sem=ss, recv_sem=rs,
-                device_id=(hme, p), device_id_type=MESH,
-            ).start()
-            return carry
-
-        lax.fori_loop(0, NS - 1, step, 0)
+        each_peer(lambda p: send(src_at(p), dst.at[me], ss, rs, (hme, p)))
 
     def send_heads(src, dst, ss, rs):
-        def step(i, carry):
-            pltpu.make_async_remote_copy(
-                src_ref=src, dst_ref=dst.at[hme], send_sem=ss, recv_sem=rs,
-                device_id=((hme + 1 + i) % NH, me), device_id_type=MESH,
-            ).start()
-            return carry
-
-        lax.fori_loop(0, NH - 1, step, 0)
+        each_head(lambda p: send(src, dst.at[hme], ss, rs, (p, me)))
 
     def wait_blocks(buf, n, sem):
         part = buf.at[pl.ds(0, n)]
@@ -135,7 +127,7 @@
         cnt_col.append(n)
         cnt_rows.append(to_row(n, eye))
         earlier.append(jnp.sum(tn(mb, mb) * before, axis=0, keepdims=True))
-    cnt_own = jnp.concatenate(cnt_rows + [jnp.zeros((8 - HL, C), F32)], axis=0).astype(BF16)
+    cnt_own = jnp.concatenate(cnt_rows, axis=0).astype(BF16)
     cnt_send[...] = cnt_own
     cnt_recv[me] = cnt_own
 
@@ -162,8 +154,8 @@
     loads[5].wait()
 
     pl.semaphore_wait(barrier, NS - 1 + NH - 1)
+    send_all(lambda p: cnt_send, cnt_recv, cnt_ss, cnt_rs)
     send_heads(sq_send, sq_recv, sq_ss, sq_rs)
-    send_all(lambda p: cnt_send, cnt_recv, cnt_ss, cnt_rs)
 
     wait_blocks(sq_recv, NH - 1, sq_rs)
     squares = jnp.sum(sq_recv[...], axis=0)
@@ -181,11 +173,13 @@
         xs[h, T : 2 * T, :] = k_low[:, h * HD : (h + 1) * HD]
 
     wait_blocks(cnt_recv, NS - 1, cnt_rs)
-    table = cnt_recv[...].astype(F32).reshape(ROWS, C).astype(BF16)
+    table = jnp.concatenate([cnt_recv[...].astype(F32), jnp.zeros((NS, 8 - HL, C), F32)], axis=1)
+    table = table.reshape(ROWS, C).astype(BF16)
     slot = (iota((T, 1), 0) % 2).astype(F32)
     label_col, label_row, pick_lead, pick_other, renewed_at, place_col = [], [], [], [], [], []
     mine = me.astype(F32)
     for h in range(HL):
+        g, half = h // 2, (h % 2) * 8
         spread = (iota((T, ROWS), 1) == (iota((T, ROWS), 0) // 2) * 8 + h).astype(F32).astype(BF16)
         counts = nn(spread, table)
         swing = counts - 1.0
@@ -210,9 +204,10 @@
         target = jnp.concatenate([place + 2.0 * a for a in range(4)], axis=1).astype(jnp.int32)
         onehot = (big_r == target).astype(F32).astype(BF16)
         packed = nn(onehot, xs[h])
-        f_send[h] = packed.reshape(NS, 8, HD).astype(BF16)
-        f_recv[h, me] = f_send[h, me]
-        send_all(lambda p: f_send.at[h, p], f_recv.at[h], f_ss.at[h], f_rs.at[h])
+        f_send[g, :, half : half + 8, :] = packed.reshape(NS, 8, HD).astype(BF16)
+        if half:
+            f_recv[g, me] = f_send[g, me]
+            send_all(lambda p: f_send.at[g, p], f_recv.at[g], f_ss.at[g], f_rs.at[g])
         lead_mine_row = jnp.where((other_row == 0.0) & (lead_rank_row == mine), 1.0, 0.0)
         lead_count = jnp.sum(counts * lead_mine_row, axis=1, keepdims=True)
         label = (slot < lead_count).astype(F32)
@@ -230,10 +225,8 @@
 
     factor = HD ** (-0.5)
     causal = il <= ic
-    renewed_rows = []
-    for h in range(HL):
-        wait_blocks(f_recv.at[h], NS - 1, f_rs.at[h])
-        received = f_recv[h].astype(F32).reshape(ROWS, HD).astype(BF16)
+
+    def attend(h, received):
         rows = nn(perm[...], received)
         k_wide = rows[T : 2 * T]
         u_wide = rows[3 * T : 4 * T]
@@ -251,43 +244,90 @@
         grad_q = nn(grad_scores, kr).astype(BF16)
         grad_k = tn(grad_scores, qr).astype(BF16)
         grad_v = tn(weights_low, ur).astype(BF16)
-        back = nn(permt[...], jnp.concatenate([attended, grad_q, grad_k, grad_v], axis=0))
-        b_send[h] = back.reshape(NS, 8, HD).astype(BF16)
-        b_recv[h, me] = b_send[h, me]
-        send_all(lambda p: b_send.at[h, p], b_recv.at[h], b_ss.at[h], b_rs.at[h])
         unit = k_wide * lax.rsqrt(jnp.sum(k_wide * k_wide, axis=1, keepdims=True) + EPSILON)
         lead_sum = jnp.sum(unit * label_col[h], axis=0, keepdims=True)
         other_sum = jnp.sum(unit * (1.0 - label_col[h]), axis=0, keepdims=True)
         current = cen_s[h]
+        renewed = []
         for chosen, total in ((pick_lead[h], lead_sum), (pick_other[h], other_sum)):
             blended = RETAIN * jnp.sum(current * chosen, axis=0, keepdims=True) + (1.0 - RETAIN) * total
-            renewed_rows.append(
-                blended * lax.rsqrt(jnp.sum(blended * blended, axis=1, keepdims=True) + EPSILON)
-            )
-    cen_own = jnp.concatenate(renewed_rows, axis=0).astype(BF16)
+            renewed.append(blended * lax.rsqrt(jnp.sum(blended * blended, axis=1, keepdims=True) + EPSILON))
+        return attended, grad_q, grad_k, grad_v, renewed
+
+    def by_device(arrays):
+        return nn(permt[...], jnp.concatenate(arrays, axis=0)).reshape(NS, 8, HD).astype(BF16)
+
+    def arrived(part):
+        return part.astype(F32).reshape(ROWS, HD).astype(BF16)
+
+    wait_blocks(f_recv.at[0], NS - 1, f_rs.at[0])
+    cen_rows = []
+    for h in range(2):
+        attended, grad_q, grad_k, grad_v, renewed = attend(h, arrived(f_recv[0, :, h * 8 : h * 8 + 8, :]))
+        cen_rows += renewed
+        b_send[:, h * 8 : h * 8 + 8, :] = by_device([attended, grad_q, grad_k, grad_v])
+    b_recv[me] = b_send[me]
+    send_all(lambda p: b_send.at[p], b_recv, b_ss, b_rs)
+
+    wait_blocks(f_recv.at[1], NS - 1, f_rs.at[1])
+    first, second = [], []
+    for h in range(2):
+        attended, grad_q, grad_k, grad_v, renewed = attend(h + 2, arrived(f_recv[1, :, h * 8 : h * 8 + 8, :]))
+        cen_rows += renewed
+        first += [grad_q, grad_k]
+        second += [attended, grad_v]
+    cen_own = jnp.concatenate(cen_rows, axis=0).astype(BF16)
     cen_send[...] = cen_own
-    cen_recv[me] = cen_own
-    send_all(lambda p: cen_send, cen_recv, cen_ss, cen_rs)
+    cen_recv[my_x, my_z] = cen_own
+    w_send[0] = by_device(first)
+    w_recv[0, me] = w_send[0, me]
+
+    def cen_along_z(i, carry):
+        send(cen_send, cen_recv.at[my_x, my_z], cen_ss, cen_rs, (hme, my_x * NZ + (my_z + 1 + i) % NZ))
+        return carry
+
+    lax.fori_loop(0, NZ - 1, cen_along_z, 0)
+    send_all(lambda p: w_send.at[0, p], w_recv.at[0], w_ss.at[0], w_rs.at[0])
+    w_send[1] = by_device(second)
+    w_recv[1, me] = w_send[1, me]
+    send_all(lambda p: w_send.at[1, p], w_recv.at[1], w_ss.at[1], w_rs.at[1])
 
     q_inner = jnp.zeros((T, 1), F32)
     k_inner = jnp.zeros((T, 1), F32)
-    for h in range(HL):
+
+    def keep_grads(h, grad_q, grad_k, q_sum, k_sum):
         cols = slice(h * HD, (h + 1) * HD)
-        wait_blocks(b_recv.at[h], NS - 1, b_rs.at[h])
-        received = b_recv[h].astype(F32).reshape(ROWS, HD).astype(BF16)
-        home = nn(oht[h], received)
+        gql_s[:, cols] = grad_q
+        gkl_s[:, cols] = grad_k
+        return (
+            q_sum + jnp.sum(grad_q * qn_s[:, cols], axis=1, keepdims=True),
+            k_sum + jnp.sum(grad_k * kn_s[:, cols], axis=1, keepdims=True),
+        )
+
+    wait_blocks(b_recv, NS - 1, b_rs)
+    for h in range(2):
+        cols = slice(h * HD, (h + 1) * HD)
+        home = nn(oht[h], arrived(b_recv[:, h * 8 : h * 8 + 8, :]))
         att_o[:, cols] = home[0:T].astype(BF16)
         gv_o[:, cols] = home[3 * T : 4 * T].astype(BF16)
-        gql_s[:, cols] = home[T : 2 * T]
-        gkl_s[:, cols] = home[2 * T : 3 * T]
-        q_inner += jnp.sum(home[T : 2 * T] * qn_s[:, cols], axis=1, keepdims=True)
-        k_inner += jnp.sum(home[2 * T : 3 * T] * kn_s[:, cols], axis=1, keepdims=True)
+        q_inner, k_inner = keep_grads(h, home[T : 2 * T], home[2 * T : 3 * T], q_inner, k_inner)
+
+    wait_blocks(cen_recv.at[my_x], NZ - 1, cen_rs)
+    for e in range(NX - 1):
+        send(cen_recv.at[my_x], cen_recv.at[my_x], cex_ss, cex_rs, (hme, row_of[e] + my_z))
+
+    wait_blocks(w_recv.at[0], NS - 1, w_rs.at[0])
+    received = arrived(w_recv[0])
+    for h in range(2, HL):
+        two = slice((h - 2) * 2 * T, (h - 1) * 2 * T)
+        home = nn(oht[h, two, :], received)
+        q_inner, k_inner = keep_grads(h, home[0:T], home[T : 2 * T], q_inner, k_inner)
     in_own = jnp.concatenate([to_row(q_inner, eye), to_row(k_inner, eye), jnp.zeros((6, T), F32)], axis=0)
     in_send[...] = in_own
     in_recv[hme] = in_own
     send_heads(in_send, in_recv, in_ss, in_rs)
 
-    wait_blocks(cen_recv, NS - 1, cen_rs)
+    wait_blocks(cen_recv, NX - 1, cex_rs)
     renewed = cen_recv[...].astype(F32).reshape(ROWS, HD).astype(BF16)
     for h in range(HL):
         gather = (iota((C, ROWS), 1) == renewed_at[h]).astype(F32).astype(BF16)
@@ -303,20 +343,39 @@
     wait_blocks(sq_recv, NH - 1, sq_ss)
     wait_blocks(in_recv, NH - 1, in_ss)
     wait_blocks(cnt_recv, NS - 1, cnt_ss)
-    wait_blocks(cen_recv, NS - 1, cen_ss)
-    for h in range(HL):
-        wait_blocks(f_send.at[h], NS - 1, f_ss.at[h])
-        wait_blocks(b_send.at[h], NS - 1, b_ss.at[h])
+    wait_blocks(cen_recv.at[my_x], NZ - 1, cen_ss)
+    wait_blocks(cen_recv, NX - 1, cex_ss)
+    for g in range(2):
+        wait_blocks(f_send.at[g], NS - 1, f_ss.at[g])
+        wait_blocks(w_send.at[g], NS - 1, w_ss.at[g])
+    wait_blocks(b_send, NS - 1, b_ss)
+
+    wait_blocks(w_recv.at[1], NS - 1, w_rs.at[1])
+    received = arrived(w_recv[1])
+    for h in range(2, HL):
+        cols = slice(h * HD, (h + 1) * HD)
+        two = slice((h - 2) * 2 * T, (h - 1) * 2 * T)
+        home = nn(oht[h, two, :], received)
+        att_o[:, cols] = home[0:T].astype(BF16)
+        gv_o[:, cols] = home[T : 2 * T].astype(BF16)
+
+
+def put_out(*refs):
+    n = len(refs) // 2
+    sems = refs[-1]
+    copies = [pltpu.make_async_copy(refs[i], refs[n + i], sems.at[i]) for i in range(n)]
+    for copy in copies:
+        copy.start()
+    for copy in copies:
+        copy.wait()
 
 
 def local(query_vectors, key_vectors, value_vectors, cluster, centroids, upstream):
     wide = (T, HL * HD)
-    blocks = (HL, NS, 8, HD)
     dma = pltpu.SemaphoreType.DMA
-    return pl.pallas_call(
+    held = pl.pallas_call(
         kernel,
-        out_shape=tuple(jax.ShapeDtypeStruct(wide, BF16) for _ in range(4))
-        + (jax.ShapeDtypeStruct((HL, C, HD), F32),),
+        out_shape=tuple(pltpu.VMEM(wide, BF16) for _ in range(4)) + (pltpu.VMEM((HL, C, HD), F32),),
         in_specs=[pl.BlockSpec(memory_space=pl.ANY)] * 6,
         out_specs=tuple([pl.BlockSpec(memory_space=pltpu.VMEM)] * 5),
         scratch_shapes=[
@@ -327,14 +386,24 @@
             pltpu.VMEM((ROWS, ROWS), BF16), pltpu.VMEM((ROWS, ROWS), BF16), pltpu.VMEM((HL, ROWS, ROWS), BF16),
             pltpu.VMEM((8, T), F32), pltpu.VMEM((NH, 8, T), F32),
             pltpu.VMEM((8, T), F32), pltpu.VMEM((NH, 8, T), F32),
-            pltpu.VMEM((8, C), BF16), pltpu.VMEM((NS, 8, C), BF16),
-            pltpu.VMEM((8, HD), BF16), pltpu.VMEM((NS, 8, HD), BF16),
-            pltpu.VMEM(blocks, BF16), pltpu.VMEM(blocks, BF16), pltpu.VMEM(blocks, BF16), pltpu.VMEM(blocks, BF16),
-            dma((6,)), dma, dma, dma, dma, dma, dma, dma, dma,
-            dma((HL,)), dma((HL,)), dma((HL,)), dma((HL,)),
+            pltpu.VMEM((HL, C), BF16), pltpu.VMEM((NS, HL, C), BF16),
+            pltpu.VMEM((8, HD), BF16), pltpu.VMEM((NX, NZ, 8, HD), BF16),
+            pltpu.VMEM((2, NS, 16, HD), BF16), pltpu.VMEM((2, NS, 16, HD), BF16),
+            pltpu.VMEM((NS, 16, HD), BF16), pltpu.VMEM((NS, 16, HD), BF16),
+            pltpu.VMEM((2, NS, 8, HD), BF16), pltpu.VMEM((2, NS, 8, HD), BF16),
+            dma((6,)), dma, dma, dma, dma, dma, dma, dma, dma, dma, dma,
+            dma((2,)), dma((2,)), dma, dma, dma((2,)), dma((2,)),
         ],
         compiler_params=pltpu.CompilerParams(collective_id=0, has_side_effects=True),
     )(query_vectors, key_vectors, value_vectors, upstream, cluster, centroids)
+    return pl.pallas_call(
+        put_out,
+        out_shape=tuple(jax.ShapeDtypeStruct(wide, BF16) for _ in range(4))
+        + (jax.ShapeDtypeStruct((HL, C, HD), F32),),
+        in_specs=[pl.BlockSpec(memory_space=pltpu.VMEM)] * 5,
+        out_specs=tuple([pl.BlockSpec(memory_space=pl.ANY)] * 5),
+        scratch_shapes=[dma((5,))],
+    )(*(pltpu.with_memory_space_constraint(one, pltpu.VMEM) for one in held))
 
 
 def solution(mesh):

time: 93.6 us -> 80.7 us (0.86)
  Pallas kernels: 88.2 us -> 79.9 us
  local copies, waits for them, and re-layouts: 4.58 us -> 0 us
    pallas_call x1 -> x2, Pallas kernels: 88.2 us -> 79.9 us  [the longest x1 79 us: local(): pl.pallas_call(kernel, out_shape=tuple((pltpu.VMEM(wide, BF16) for _ in r...]
    unnamed x13 -> x0, local copies, waits for them, and re-layouts: 4.58 us -> none
where the time goes in v2:
time: 80.7 us; the launch traced here: 80.6 us
  Pallas kernels  79.9 us (99%)
    pallas_call x1, Pallas kernels, local(): pl.pallas_call(kernel, out_shape=tuple((pltpu.VMEM(wide, BF16) for _ in r...  79 us

profile of v2, /device:TPU:1, one launch (start us, length us, event | category | flops | bytes accessed | tf_op | source)
XLA Modules:
  0.0 80.6 jit_solution(18093846293977312351)
XLA Ops:
  0.6 79.0 %shard_map.101 = (bf16[128,512]{1,0:T(8,128)(2,1)S(1)}, bf16[128,512]{1,0:T(8,128)(2,1)S(1)}, bf16[128,512]{1,0:T(8,128)(2,1)S(1)}, bf16[128,512]{1,0:T(8,128)(2,1)S(1)}, f32[4,128,128]{2,1,0:T(8,128)S(1)}) custom-call(bf16[128,512]{1,0:T(8,128)(2,1)} %q_hbm.1, bf16[128,512]{1,0:T(8,128)(2,1)} %k_hbm.1, bf16[128,512]{1,0:T(8,128)(2,1)} %v_hbm.1, ...), custom_call_target="tpu_custom_call" | custom-call | tf_op jit(solution)/shard_map/pallas_call | solution.py:376
  79.6 0.9 %shard_map.102 = (bf16[128,512]{1,0:T(8,128)(2,1)}, bf16[128,512]{1,0:T(8,128)(2,1)}, bf16[128,512]{1,0:T(8,128)(2,1)}, bf16[128,512]{1,0:T(8,128)(2,1)}, f32[4,128,128]{2,1,0:T(8,128)}) custom-call(bf16[128,512]{1,0:T(8,128)(2,1)S(1)} %get-tuple-element.10.refs_0_, bf16[128,512]{1,0:T(8,128)(2,1)S(1)} %get-tuple-element.11.refs_1_, ...), custom_call_target="tpu_custom_call" | custom-call | tf_op jit(solution)/shard_map/pallas_call | solution.py:399

commit v3 on v2

--- a/solution.py
+++ b/solution.py
@@ -22,6 +22,9 @@
 T = 128
 C = 128
 WIDTH = 4096
+NEAR = 4
+SPLIT = 3
+LATER = 5
 ROWS = NS * 8
 
 
@@ -55,16 +58,16 @@
     q_s, k_s, v_s, u_s, cl_s, cen_s,
     xs, qn_s, kn_s, gql_s, gkl_s, perm, permt, oht,
     sq_send, sq_recv, in_send, in_recv, cnt_send, cnt_recv, cen_send, cen_recv,
-    f_send, f_recv, b_send, b_recv, w_send, w_recv,
+    f_send, f_recv, w_send, w_recv,
     load_sem, sq_ss, sq_rs, in_ss, in_rs, cnt_ss, cnt_rs, cen_ss, cen_rs, cex_ss, cex_rs,
-    f_ss, f_rs, b_ss, b_rs, w_ss, w_rs,
+    f_ss, f_rs, w_ss, w_rs,
 ):
     me = lax.axis_index("seq")
     hme = lax.axis_index("head")
     my_x, my_z = me // NZ, me % NZ
     row_of = [((my_x + NX - 1 - e) % NX) * NZ for e in range(NX)]
 
-    def each_peer(act):
+    def each_peer(act, begin=0, end=NZ):
         def step(j, carry):
             far = NZ // 2 - (j + 1) // 2
             z = (my_z + far * (2 * (j % 2) - 1) + NZ) % NZ
@@ -72,9 +75,10 @@
                 act(row_of[e] + z)
             return carry
 
-        lax.fori_loop(0, NZ - 1, step, 0)
-        for e in range(NX - 1):
-            act(row_of[e] + my_z)
+        lax.fori_loop(begin, min(end, NZ - 1), step, 0)
+        if end == NZ:
+            for e in range(NX - 1):
+                act(row_of[e] + my_z)
 
     def each_head(act):
         def step(i, carry):
@@ -84,8 +88,16 @@
         lax.fori_loop(0, NH - 1, step, 0)
 
     barrier = pltpu.get_barrier_semaphore()
-    each_peer(lambda p: pl.semaphore_signal(barrier, 1, device_id=(hme, p), device_id_type=MESH))
-    each_head(lambda p: pl.semaphore_signal(barrier, 1, device_id=(p, me), device_id_type=MESH))
+
+    def greet(to):
+        pl.semaphore_signal(barrier, 1, device_id=to, device_id_type=MESH)
+
+    for d in range(NEAR, 0, -1):
+        for side in (d, NZ - d):
+            greet((hme, my_x * NZ + (my_z + side) % NZ))
+    for e in range(NX - 1):
+        greet((hme, row_of[e] + my_z))
+    each_head(lambda p: greet((p, me)))
 
     loads = [
         pltpu.make_async_copy(src, dst, load_sem.at[n])
@@ -101,8 +113,8 @@
             src_ref=src, dst_ref=dst, send_sem=ss, recv_sem=rs, device_id=to, device_id_type=MESH
         ).start()
 
-    def send_all(src_at, dst, ss, rs):
-        each_peer(lambda p: send(src_at(p), dst.at[me], ss, rs, (hme, p)))
+    def send_all(src_at, dst, ss, rs, begin=0, end=NZ):
+        each_peer(lambda p: send(src_at(p), dst.at[me], ss, rs, (hme, p)), begin, end)
 
     def send_heads(src, dst, ss, rs):
         each_head(lambda p: send(src, dst.at[hme], ss, rs, (p, me)))
@@ -129,7 +141,7 @@
         earlier.append(jnp.sum(tn(mb, mb) * before, axis=0, keepdims=True))
     cnt_own = jnp.concatenate(cnt_rows, axis=0).astype(BF16)
     cnt_send[...] = cnt_own
-    cnt_recv[me] = cnt_own
+    cnt_recv[my_x, my_z] = cnt_own
 
     loads[1].wait()
     loads[2].wait()
@@ -137,7 +149,7 @@
     q_row = to_row(jnp.sum(qf * qf, axis=1, keepdims=True), eye)
     kf = k_s[...].astype(F32)
     k_row = to_row(jnp.sum(kf * kf, axis=1, keepdims=True), eye)
-    sq_own = jnp.concatenate([q_row, k_row, jnp.zeros((6, T), F32)], axis=0)
+    sq_own = jnp.concatenate([q_row, k_row], axis=0)
     sq_send[...] = sq_own
     sq_recv[hme] = sq_own
 
@@ -153,27 +165,43 @@
         xs[h, 3 * T : 4 * T, :] = u_s[:, h * HD : (h + 1) * HD]
     loads[5].wait()
 
-    pl.semaphore_wait(barrier, NS - 1 + NH - 1)
-    send_all(lambda p: cnt_send, cnt_recv, cnt_ss, cnt_rs)
+    pl.semaphore_wait(barrier, 2 * NEAR + NX - 1 + NH - 1)
+    for d in range(NEAR, 0, -1):
+        for side in (d, NZ - d):
+            to = (hme, my_x * NZ + (my_z + side) % NZ)
+            send(cnt_send, cnt_recv.at[my_x, my_z], cnt_ss.at[0], cnt_rs.at[0], to)
     send_heads(sq_send, sq_recv, sq_ss, sq_rs)
 
-    wait_blocks(sq_recv, NH - 1, sq_rs)
-    squares = jnp.sum(sq_recv[...], axis=0)
-    scales = lax.rsqrt(squares * (1.0 / WIDTH) + EPSILON)
-    q_scale = to_col(scales[0:1, :], eye)
-    k_scale = to_col(scales[1:2, :], eye)
-    q_norm = q_s[...].astype(F32) * q_scale
-    k_norm = k_s[...].astype(F32) * k_scale
-    qn_s[...] = q_norm
-    kn_s[...] = k_norm
-    q_low = q_norm.astype(BF16)
-    k_low = k_norm.astype(BF16)
-    for h in range(HL):
-        xs[h, 0:T, :] = q_low[:, h * HD : (h + 1) * HD]
-        xs[h, T : 2 * T, :] = k_low[:, h * HD : (h + 1) * HD]
-
-    wait_blocks(cnt_recv, NS - 1, cnt_rs)
-    table = jnp.concatenate([cnt_recv[...].astype(F32), jnp.zeros((NS, 8 - HL, C), F32)], axis=1)
+    def normalize():
+        wait_blocks(sq_recv, NH - 1, sq_rs)
+        squares = jnp.sum(sq_recv[...], axis=0)
+        scales = lax.rsqrt(squares * (1.0 / WIDTH) + EPSILON)
+        q_scale = to_col(scales[0:1, :], eye)
+        k_scale = to_col(scales[1:2, :], eye)
+        q_norm = q_s[...].astype(F32) * q_scale
+        k_norm = k_s[...].astype(F32) * k_scale
+        qn_s[...] = q_norm
+        kn_s[...] = k_norm
+        q_low = q_norm.astype(BF16)
+        k_low = k_norm.astype(BF16)
+        for h in range(HL):
+            xs[h, 0:T, :] = q_low[:, h * HD : (h + 1) * HD]
+            xs[h, T : 2 * T, :] = k_low[:, h * HD : (h + 1) * HD]
+        return q_scale, k_scale
+
+    wait_blocks(cnt_recv.at[0], 2 * NEAR, cnt_rs.at[0])
+    for side, rows in ((NZ - NEAR, range(NEAR, 0, -1)), (NEAR, range(NZ - NEAR + 1, NZ))):
+        to = (hme, my_x * NZ + (my_z + side) % NZ)
+        for r in rows:
+            part = cnt_recv.at[my_x, (my_z + r) % NZ]
+            send(part, part, cnt_ss.at[1], cnt_rs.at[1], to)
+    q_scale, k_scale = normalize()
+    wait_blocks(cnt_recv.at[0], 2 * NEAR - 1, cnt_rs.at[1])
+    for e in range(NX - 1):
+        send(cnt_recv.at[my_x], cnt_recv.at[my_x], cnt_ss.at[2], cnt_rs.at[2], (hme, row_of[e] + my_z))
+    wait_blocks(cnt_recv, NX - 1, cnt_rs.at[2])
+    table = cnt_recv[...].astype(F32).reshape(NS, HL, C)
+    table = jnp.concatenate([table, jnp.zeros((NS, 8 - HL, C), F32)], axis=1)
     table = table.reshape(ROWS, C).astype(BF16)
     slot = (iota((T, 1), 0) % 2).astype(F32)
     label_col, label_row, pick_lead, pick_other, renewed_at, place_col = [], [], [], [], [], []
@@ -260,72 +288,78 @@
     def arrived(part):
         return part.astype(F32).reshape(ROWS, HD).astype(BF16)
 
-    wait_blocks(f_recv.at[0], NS - 1, f_rs.at[0])
+    def put_back(n, arrays):
+        w_send[n] = by_device(arrays)
+        w_recv[n, me] = w_send[n, me]
+
+    def send_back(n, begin=0, end=NZ):
+        send_all(lambda p: w_send.at[n, p], w_recv.at[n], w_ss.at[n], w_rs.at[n], begin, end)
+
     cen_rows = []
-    for h in range(2):
-        attended, grad_q, grad_k, grad_v, renewed = attend(h, arrived(f_recv[0, :, h * 8 : h * 8 + 8, :]))
-        cen_rows += renewed
-        b_send[:, h * 8 : h * 8 + 8, :] = by_device([attended, grad_q, grad_k, grad_v])
-    b_recv[me] = b_send[me]
-    send_all(lambda p: b_send.at[p], b_recv, b_ss, b_rs)
-
-    wait_blocks(f_recv.at[1], NS - 1, f_rs.at[1])
-    first, second = [], []
-    for h in range(2):
-        attended, grad_q, grad_k, grad_v, renewed = attend(h + 2, arrived(f_recv[1, :, h * 8 : h * 8 + 8, :]))
-        cen_rows += renewed
-        first += [grad_q, grad_k]
-        second += [attended, grad_v]
+    for g in range(2):
+        wait_blocks(f_recv.at[g], NS - 1, f_rs.at[g])
+        first, second = [], []
+        for half in range(2):
+            attended, grad_q, grad_k, grad_v, renewed = attend(
+                2 * g + half, arrived(f_recv[g, :, half * 8 : half * 8 + 8, :])
+            )
+            cen_rows += renewed
+            first += [grad_q, grad_k]
+            second += [attended, grad_v]
+        put_back(g, first)
+        send_back(g)
+        put_back(2 + g, second)
+        if g == 0:
+            send_back(2, 0, SPLIT)
     cen_own = jnp.concatenate(cen_rows, axis=0).astype(BF16)
     cen_send[...] = cen_own
     cen_recv[my_x, my_z] = cen_own
-    w_send[0] = by_device(first)
-    w_recv[0, me] = w_send[0, me]
 
     def cen_along_z(i, carry):
-        send(cen_send, cen_recv.at[my_x, my_z], cen_ss, cen_rs, (hme, my_x * NZ + (my_z + 1 + i) % NZ))
+        far = NZ // 2 - (i + 1) // 2
+        z = (my_z + far * (2 * (i % 2) - 1) + NZ) % NZ
+        send(cen_send, cen_recv.at[my_x, my_z], cen_ss, cen_rs, (hme, my_x * NZ + z))
         return carry
 
     lax.fori_loop(0, NZ - 1, cen_along_z, 0)
-    send_all(lambda p: w_send.at[0, p], w_recv.at[0], w_ss.at[0], w_rs.at[0])
-    w_send[1] = by_device(second)
-    w_recv[1, me] = w_send[1, me]
-    send_all(lambda p: w_send.at[1, p], w_recv.at[1], w_ss.at[1], w_rs.at[1])
-
-    q_inner = jnp.zeros((T, 1), F32)
-    k_inner = jnp.zeros((T, 1), F32)
-
-    def keep_grads(h, grad_q, grad_k, q_sum, k_sum):
-        cols = slice(h * HD, (h + 1) * HD)
-        gql_s[:, cols] = grad_q
-        gkl_s[:, cols] = grad_k
-        return (
-            q_sum + jnp.sum(grad_q * qn_s[:, cols], axis=1, keepdims=True),
-            k_sum + jnp.sum(grad_k * kn_s[:, cols], axis=1, keepdims=True),
-        )
-
-    wait_blocks(b_recv, NS - 1, b_rs)
-    for h in range(2):
-        cols = slice(h * HD, (h + 1) * HD)
-        home = nn(oht[h], arrived(b_recv[:, h * 8 : h * 8 + 8, :]))
-        att_o[:, cols] = home[0:T].astype(BF16)
-        gv_o[:, cols] = home[3 * T : 4 * T].astype(BF16)
-        q_inner, k_inner = keep_grads(h, home[T : 2 * T], home[2 * T : 3 * T], q_inner, k_inner)
+    send_back(2, SPLIT, NZ)
+
+    inner_sums = [jnp.zeros((T, 1), F32), jnp.zeros((T, 1), F32)]
+
+    def home_grads(g, received):
+        for half in range(2):
+            h = 2 * g + half
+            cols = slice(h * HD, (h + 1) * HD)
+            home = nn(oht[h, half * 2 * T : (half + 1) * 2 * T, :], received)
+            gql_s[:, cols] = home[0:T]
+            gkl_s[:, cols] = home[T : 2 * T]
+            inner_sums[0] += jnp.sum(home[0:T] * qn_s[:, cols], axis=1, keepdims=True)
+            inner_sums[1] += jnp.sum(home[T : 2 * T] * kn_s[:, cols], axis=1, keepdims=True)
+
+    def home_values(g, received):
+        for half in range(2):
+            h = 2 * g + half
+            cols = slice(h * HD, (h + 1) * HD)
+            home = nn(oht[h, half * 2 * T : (half + 1) * 2 * T, :], received)
+            att_o[:, cols] = home[0:T].astype(BF16)
+            gv_o[:, cols] = home[T : 2 * T].astype(BF16)
+
+    wait_blocks(w_recv.at[0], NS - 1, w_rs.at[0])
+    home_grads(0, arrived(w_recv[0]))
+    wait_blocks(w_recv.at[1], NS - 1, w_rs.at[1])
+    home_grads(1, arrived(w_recv[1]))
+    in_own = jnp.concatenate([to_row(inner_sums[0], eye), to_row(inner_sums[1], eye)], axis=0)
+    in_send[...] = in_own
+    in_recv[hme] = in_own
+    send_heads(in_send, in_recv, in_ss, in_rs)
+    send_back(3, 0, LATER)
 
     wait_blocks(cen_recv.at[my_x], NZ - 1, cen_rs)
     for e in range(NX - 1):
         send(cen_recv.at[my_x], cen_recv.at[my_x], cex_ss, cex_rs, (hme, row_of[e] + my_z))
-
-    wait_blocks(w_recv.at[0], NS - 1, w_rs.at[0])
-    received = arrived(w_recv[0])
-    for h in range(2, HL):
-        two = slice((h - 2) * 2 * T, (h - 1) * 2 * T)
-        home = nn(oht[h, two, :], received)
-        q_inner, k_inner = keep_grads(h, home[0:T], home[T : 2 * T], q_inner, k_inner)
-    in_own = jnp.concatenate([to_row(q_inner, eye), to_row(k_inner, eye), jnp.zeros((6, T), F32)], axis=0)
-    in_send[...] = in_own
-    in_recv[hme] = in_own
-    send_heads(in_send, in_recv, in_ss, in_rs)
+    send_back(3, LATER, NZ)
+    wait_blocks(w_recv.at[2], NS - 1, w_rs.at[2])
+    home_values(0, arrived(w_recv[2]))
 
     wait_blocks(cen_recv, NX - 1, cex_rs)
     renewed = cen_recv[...].astype(F32).reshape(ROWS, HD).astype(BF16)
@@ -342,22 +376,20 @@
 
     wait_blocks(sq_recv, NH - 1, sq_ss)
     wait_blocks(in_recv, NH - 1, in_ss)
-    wait_blocks(cnt_recv, NS - 1, cnt_ss)
+    wait_blocks(cnt_recv.at[0], 2 * NEAR, cnt_ss.at[0])
+    wait_blocks(cnt_recv.at[0], 2 * NEAR - 1, cnt_ss.at[1])
+    wait_blocks(cnt_recv, NX - 1, cnt_ss.at[2])
     wait_blocks(cen_recv.at[my_x], NZ - 1, cen_ss)
     wait_blocks(cen_recv, NX - 1, cex_ss)
     for g in range(2):
         wait_blocks(f_send.at[g], NS - 1, f_ss.at[g])
-        wait_blocks(w_send.at[g], NS - 1, w_ss.at[g])
-    wait_blocks(b_send, NS - 1, b_ss)
-
-    wait_blocks(w_recv.at[1], NS - 1, w_rs.at[1])
-    received = arrived(w_recv[1])
-    for h in range(2, HL):
-        cols = slice(h * HD, (h + 1) * HD)
-        two = slice((h - 2) * 2 * T, (h - 1) * 2 * T)
-        home = nn(oht[h, two, :], received)
-        att_o[:, cols] = home[0:T].astype(BF16)
-        gv_o[:, cols] = home[T : 2 * T].astype(BF16)
+
+    for n in range(3):
+        wait_blocks(w_send.at[n], NS - 1, w_ss.at[n])
+
+    wait_blocks(w_recv.at[3], NS - 1, w_rs.at[3])
+    home_values(1, arrived(w_recv[3]))
+    wait_blocks(w_send.at[3], NS - 1, w_ss.at[3])
 
 
 def put_out(*refs):
@@ -384,15 +416,14 @@
             pltpu.VMEM((HL, 4 * T, HD), BF16), pltpu.VMEM(wide, F32), pltpu.VMEM(wide, F32),
             pltpu.VMEM(wide, F32), pltpu.VMEM(wide, F32),
             pltpu.VMEM((ROWS, ROWS), BF16), pltpu.VMEM((ROWS, ROWS), BF16), pltpu.VMEM((HL, ROWS, ROWS), BF16),
-            pltpu.VMEM((8, T), F32), pltpu.VMEM((NH, 8, T), F32),
-            pltpu.VMEM((8, T), F32), pltpu.VMEM((NH, 8, T), F32),
-            pltpu.VMEM((HL, C), BF16), pltpu.VMEM((NS, HL, C), BF16),
+            pltpu.VMEM((2, T), F32), pltpu.VMEM((NH, 2, T), F32),
+            pltpu.VMEM((2, T), F32), pltpu.VMEM((NH, 2, T), F32),
+            pltpu.VMEM((HL, C), BF16), pltpu.VMEM((NX, NZ, HL, C), BF16),
             pltpu.VMEM((8, HD), BF16), pltpu.VMEM((NX, NZ, 8, HD), BF16),
             pltpu.VMEM((2, NS, 16, HD), BF16), pltpu.VMEM((2, NS, 16, HD), BF16),
-            pltpu.VMEM((NS, 16, HD), BF16), pltpu.VMEM((NS, 16, HD), BF16),
-            pltpu.VMEM((2, NS, 8, HD), BF16), pltpu.VMEM((2, NS, 8, HD), BF16),
-            dma((6,)), dma, dma, dma, dma, dma, dma, dma, dma, dma, dma,
-            dma((2,)), dma((2,)), dma, dma, dma((2,)), dma((2,)),
+            pltpu.VMEM((4, NS, 8, HD), BF16), pltpu.VMEM((4, NS, 8, HD), BF16),
+            dma((6,)), dma, dma, dma, dma, dma((3,)), dma((3,)), dma, dma, dma, dma,
+            dma((2,)), dma((2,)), dma((4,)), dma((4,)),
         ],
         compiler_params=pltpu.CompilerParams(collective_id=0, has_side_effects=True),
     )(query_vectors, key_vectors, value_vectors, upstream, cluster, centroids)

time: 80.7 us -> 78.3 us (0.970)
  the two profiles are of different devices: /device:TPU:1 before, /device:TPU:6 now
where the time goes in v3:
time: 78.3 us; the launch traced here: 78.1 us
  Pallas kernels  77.5 us (99%)
    pallas_call x1, Pallas kernels, local(): pl.pallas_call(kernel, out_shape=tuple((pltpu.VMEM(wide, BF16) for _ in r...  76.6 us

profile of v3, /device:TPU:6, one launch (start us, length us, event | category | flops | bytes accessed | tf_op | source)
XLA Modules:
  0.0 78.1 jit_solution(3491278707521191440)
XLA Ops:
  0.6 76.6 %shard_map.101 = (bf16[128,512]{1,0:T(8,128)(2,1)S(1)}, bf16[128,512]{1,0:T(8,128)(2,1)S(1)}, bf16[128,512]{1,0:T(8,128)(2,1)S(1)}, bf16[128,512]{1,0:T(8,128)(2,1)S(1)}, f32[4,128,128]{2,1,0:T(8,128)S(1)}) custom-call(bf16[128,512]{1,0:T(8,128)(2,1)} %q_hbm.1, bf16[128,512]{1,0:T(8,128)(2,1)} %k_hbm.1, bf16[128,512]{1,0:T(8,128)(2,1)} %v_hbm.1, ...), custom_call_target="tpu_custom_call" | custom-call | tf_op jit(solution)/shard_map/pallas_call | solution.py:408
  77.2 0.9 %shard_map.102 = (bf16[128,512]{1,0:T(8,128)(2,1)}, bf16[128,512]{1,0:T(8,128)(2,1)}, bf16[128,512]{1,0:T(8,128)(2,1)}, bf16[128,512]{1,0:T(8,128)(2,1)}, f32[4,128,128]{2,1,0:T(8,128)}) custom-call(bf16[128,512]{1,0:T(8,128)(2,1)S(1)} %get-tuple-element.10.refs_0_, bf16[128,512]{1,0:T(8,128)(2,1)S(1)} %get-tuple-element.11.refs_1_, ...), custom_call_target="tpu_custom_call" | custom-call | tf_op jit(solution)/shard_map/pallas_call | solution.py:430

commit v4 on v3

--- a/solution.py
+++ b/solution.py
@@ -23,8 +23,7 @@
 C = 128
 WIDTH = 4096
 NEAR = 4
-SPLIT = 3
-LATER = 5
+LATER = 11
 ROWS = NS * 8
 
 
@@ -143,6 +142,12 @@
     cnt_send[...] = cnt_own
     cnt_recv[my_x, my_z] = cnt_own
 
+    pl.semaphore_wait(barrier, 2 * NEAR + NX - 1 + NH - 1)
+    for d in range(NEAR, 0, -1):
+        for side in (d, NZ - d):
+            to = (hme, my_x * NZ + (my_z + side) % NZ)
+            send(cnt_send, cnt_recv.at[my_x, my_z], cnt_ss.at[0], cnt_rs.at[0], to)
+
     loads[1].wait()
     loads[2].wait()
     qf = q_s[...].astype(F32)
@@ -152,6 +157,7 @@
     sq_own = jnp.concatenate([q_row, k_row], axis=0)
     sq_send[...] = sq_own
     sq_recv[hme] = sq_own
+    send_heads(sq_send, sq_recv, sq_ss, sq_rs)
 
     big_r = iota((ROWS, ROWS), 0)
     big_l = iota((ROWS, ROWS), 1)
@@ -164,13 +170,6 @@
         xs[h, 2 * T : 3 * T, :] = v_s[:, h * HD : (h + 1) * HD]
         xs[h, 3 * T : 4 * T, :] = u_s[:, h * HD : (h + 1) * HD]
     loads[5].wait()
-
-    pl.semaphore_wait(barrier, 2 * NEAR + NX - 1 + NH - 1)
-    for d in range(NEAR, 0, -1):
-        for side in (d, NZ - d):
-            to = (hme, my_x * NZ + (my_z + side) % NZ)
-            send(cnt_send, cnt_recv.at[my_x, my_z], cnt_ss.at[0], cnt_rs.at[0], to)
-    send_heads(sq_send, sq_recv, sq_ss, sq_rs)
 
     def normalize():
         wait_blocks(sq_recv, NH - 1, sq_rs)
@@ -309,8 +308,6 @@
         put_back(g, first)
         send_back(g)
         put_back(2 + g, second)
-        if g == 0:
-            send_back(2, 0, SPLIT)
     cen_own = jnp.concatenate(cen_rows, axis=0).astype(BF16)
     cen_send[...] = cen_own
     cen_recv[my_x, my_z] = cen_own
@@ -322,7 +319,7 @@
         return carry
 
     lax.fori_loop(0, NZ - 1, cen_along_z, 0)
-    send_back(2, SPLIT, NZ)
+    send_back(2)
 
     inner_sums = [jnp.zeros((T, 1), F32), jnp.zeros((T, 1), F32)]
 

time: 78.3 us -> 77.1 us (0.985)
  Pallas kernels: 77.5 us -> 76.3 us
    pallas_call x1, Pallas kernels: 76.6 us -> 75.4 us  [local(): pl.pallas_call(kernel, out_shape=tuple((pltpu.VMEM(wide, BF16) for _ in r...]
where the time goes in v4:
time: 77.1 us; the launch traced here: 77 us
  Pallas kernels  76.3 us (99%)
    pallas_call x1, Pallas kernels, local(): pl.pallas_call(kernel, out_shape=tuple((pltpu.VMEM(wide, BF16) for _ in r...  75.4 us

profile of v4, /device:TPU:6, one launch (start us, length us, event | category | flops | bytes accessed | tf_op | source)
XLA Modules:
  0.0 77.0 jit_solution(7797183600740624867)
XLA Ops:
  0.6 75.4 %shard_map.101 = (bf16[128,512]{1,0:T(8,128)(2,1)S(1)}, bf16[128,512]{1,0:T(8,128)(2,1)S(1)}, bf16[128,512]{1,0:T(8,128)(2,1)S(1)}, bf16[128,512]{1,0:T(8,128)(2,1)S(1)}, f32[4,128,128]{2,1,0:T(8,128)S(1)}) custom-call(bf16[128,512]{1,0:T(8,128)(2,1)} %q_hbm.1, bf16[128,512]{1,0:T(8,128)(2,1)} %k_hbm.1, bf16[128,512]{1,0:T(8,128)(2,1)} %v_hbm.1, ...), custom_call_target="tpu_custom_call" | custom-call | tf_op jit(solution)/shard_map/pallas_call | solution.py:405
  76.0 0.9 %shard_map.102 = (bf16[128,512]{1,0:T(8,128)(2,1)}, bf16[128,512]{1,0:T(8,128)(2,1)}, bf16[128,512]{1,0:T(8,128)(2,1)}, bf16[128,512]{1,0:T(8,128)(2,1)}, f32[4,128,128]{2,1,0:T(8,128)}) custom-call(bf16[128,512]{1,0:T(8,128)(2,1)S(1)} %get-tuple-element.10.refs_0_, bf16[128,512]{1,0:T(8,128)(2,1)S(1)} %get-tuple-element.11.refs_1_, ...), custom_call_target="tpu_custom_call" | custom-call | tf_op jit(solution)/shard_map/pallas_call | solution.py:427

commit v5 on v4

--- a/solution.py
+++ b/solution.py
@@ -23,6 +23,7 @@
 C = 128
 WIDTH = 4096
 NEAR = 4
+HALF = 5
 LATER = 11
 ROWS = NS * 8
 
@@ -297,6 +298,8 @@
     cen_rows = []
     for g in range(2):
         wait_blocks(f_recv.at[g], NS - 1, f_rs.at[g])
+        if g == 1:
+            send_back(0, HALF, NZ)
         first, second = [], []
         for half in range(2):
             attended, grad_q, grad_k, grad_v, renewed = attend(
@@ -306,7 +309,7 @@
             first += [grad_q, grad_k]
             second += [attended, grad_v]
         put_back(g, first)
-        send_back(g)
+        send_back(g, 0, HALF if g == 0 else NZ)
         put_back(2 + g, second)
     cen_own = jnp.concatenate(cen_rows, axis=0).astype(BF16)
     cen_send[...] = cen_own

time: 77.1 us -> 78.1 us (1.013); the launches traced: 77 us -> 77.1 us
  no operation moved by 1% of the time
where the time goes in v5:
time: 78.1 us; the launch traced here: 77.1 us
  Pallas kernels  76.5 us (98%)
    pallas_call x1, Pallas kernels, local(): pl.pallas_call(kernel, out_shape=tuple((pltpu.VMEM(wide, BF16) for _ in r...  75.6 us

profile of v5, /device:TPU:6, one launch (start us, length us, event | category | flops | bytes accessed | tf_op | source)
XLA Modules:
  0.0 77.1 jit_solution(6510411249204742245)
XLA Ops:
  0.6 75.6 %shard_map.101 = (bf16[128,512]{1,0:T(8,128)(2,1)S(1)}, bf16[128,512]{1,0:T(8,128)(2,1)S(1)}, bf16[128,512]{1,0:T(8,128)(2,1)S(1)}, bf16[128,512]{1,0:T(8,128)(2,1)S(1)}, f32[4,128,128]{2,1,0:T(8,128)S(1)}) custom-call(bf16[128,512]{1,0:T(8,128)(2,1)} %q_hbm.1, bf16[128,512]{1,0:T(8,128)(2,1)} %k_hbm.1, bf16[128,512]{1,0:T(8,128)(2,1)} %v_hbm.1, ...), custom_call_target="tpu_custom_call" | custom-call | tf_op jit(solution)/shard_map/pallas_call | solution.py:408
  76.2 0.9 %shard_map.102 = (bf16[128,512]{1,0:T(8,128)(2,1)}, bf16[128,512]{1,0:T(8,128)(2,1)}, bf16[128,512]{1,0:T(8,128)(2,1)}, bf16[128,512]{1,0:T(8,128)(2,1)}, f32[4,128,128]{2,1,0:T(8,128)}) custom-call(bf16[128,512]{1,0:T(8,128)(2,1)S(1)} %get-tuple-element.10.refs_0_, bf16[128,512]{1,0:T(8,128)(2,1)S(1)} %get-tuple-element.11.refs_1_, ...), custom_call_target="tpu_custom_call" | custom-call | tf_op jit(solution)/shard_map/pallas_call | solution.py:430
